TPU v7x, 8 devices: a whole 2x2x1 slice. The times are simulated.
8 devices in a mesh: dp: 1 (over z), tp: 2 (over y), ctx: 4 (over x, core).
Axes of the slice: x: 2, y: 2, z: 1, core: 2. Of those that a mesh axis runs over, the one named last changes fastest.
Arguments:
- hidden: bfloat16 [512, 5120], P(('dp', 'ctx'))
- w_q: bfloat16 [5120, 5120], P(None, 'tp')
- w_k: bfloat16 [5120, 1024], P(None, 'tp')
- w_v: bfloat16 [5120, 1024], P(None, 'tp')
- w_o: bfloat16 [5120, 5120], P('tp')
- k_prefix: bfloat16 [1024, 8, 128], P(('dp', 'ctx'), 'tp')
- v_prefix: bfloat16 [1024, 8, 128], P(('dp', 'ctx'), 'tp')
- k_suffix: bfloat16 [512, 256, 8, 128], P(('dp', 'ctx'), None, 'tp')
- v_suffix: bfloat16 [512, 256, 8, 128], P(('dp', 'ctx'), None, 'tp')
- seq_lens: int32 [512], P(('dp', 'ctx'))
Outputs:
- output: bfloat16 [512, 5120], P(('dp', 'ctx'))
All inputs are finite; a program needn't handle non-finite values.
Results may differ from a plain program's by a relative error of at most 0.0049065.
Values are sent between devices in bfloat16 or wider.
A program may use at most 1 GiB of HBM per device.

v0:
```python
import jax
import jax.numpy as jnp
from jax import lax
from jax.sharding import PartitionSpec as P, NamedSharding


def solution(mesh):
    ctx_size = mesh.shape['ctx']
    row_axes = ('dp', 'ctx')

    def device_step(hidden, w_q, w_k, w_v, w_o, k_prefix, v_prefix, k_suffix, v_suffix, seq_lens):
        seq_count = hidden.shape[0]
        kv_local = k_prefix.shape[1]
        head_dim = k_prefix.shape[2]
        group_size = w_q.shape[1] // (kv_local * head_dim)
        score_scale = head_dim ** -0.5
        q_local = jnp.dot(hidden, w_q, preferred_element_type=jnp.float32).astype(jnp.bfloat16)
        q_local = q_local.reshape(seq_count, kv_local, group_size, head_dim)
        k_new = jnp.dot(hidden, w_k, preferred_element_type=jnp.float32).astype(jnp.bfloat16).reshape(seq_count, kv_local, head_dim)
        v_new = jnp.dot(hidden, w_v, preferred_element_type=jnp.float32).astype(jnp.bfloat16).reshape(seq_count, kv_local, head_dim)
        q_every = lax.all_gather(q_local, 'ctx', axis=0, tiled=True)
        s_pre = jnp.einsum('bkgd,pkd->bkgp', q_every, k_prefix, preferred_element_type=jnp.float32) * score_scale
        m_pre = jnp.max(s_pre, axis=-1)
        e_pre = jnp.exp(s_pre - m_pre[..., None])
        l_pre = jnp.sum(e_pre, axis=-1)
        o_pre = jnp.einsum('bkgp,pkd->bkgd', e_pre.astype(jnp.bfloat16), v_prefix, preferred_element_type=jnp.float32)
        partial_state = jnp.concatenate([o_pre / l_pre[..., None], (m_pre + jnp.log(l_pre))[..., None]], axis=-1)
        returned = lax.all_to_all(partial_state, 'ctx', 0, 0, tiled=True)
        returned = returned.reshape(ctx_size, seq_count, kv_local, group_size, head_dim + 1)
        o_parts = returned[..., :head_dim]
        lse_parts = returned[..., head_dim]
        slot_ids = jnp.arange(k_suffix.shape[1])
        in_cache = (slot_ids[None, :] < seq_lens[:, None])[:, None, None, :]
        s_cache = jnp.einsum('bkgd,bskd->bkgs', q_local, k_suffix, preferred_element_type=jnp.float32) * score_scale
        s_cache = jnp.where(in_cache, s_cache, -jnp.inf)
        s_self = jnp.einsum('clhe,cle->clh', q_local, k_new, preferred_element_type=jnp.float32) * score_scale
        m_suf = jnp.maximum(jnp.max(s_cache, axis=-1), s_self)
        e_cache = jnp.exp(s_cache - m_suf[..., None])
        e_self = jnp.exp(s_self - m_suf)
        l_suf = jnp.sum(e_cache, axis=-1) + e_self
        o_suf = jnp.einsum('bkgs,bskd->bkgd', e_cache.astype(jnp.bfloat16), v_suffix, preferred_element_type=jnp.float32)
        o_suf = (o_suf + e_self[..., None] * v_new[:, :, None, :].astype(jnp.float32)) / l_suf[..., None]
        lse_suf = m_suf + jnp.log(l_suf)
        lse_max = jnp.maximum(jnp.max(lse_parts, axis=0), lse_suf)
        w_parts = jnp.exp(lse_parts - lse_max)
        w_suf = jnp.exp(lse_suf - lse_max)
        merged = jnp.sum(w_parts[..., None] * o_parts, axis=0) + w_suf[..., None] * o_suf
        merged = merged / (jnp.sum(w_parts, axis=0) + w_suf)[..., None]
        attn_out = merged.astype(jnp.bfloat16).reshape(seq_count, kv_local * group_size * head_dim)
        proj_part = jnp.dot(attn_out, w_o, preferred_element_type=jnp.float32)
        out_hidden = hidden.astype(jnp.float32) + lax.psum(proj_part, 'tp')
        return out_hidden.astype(jnp.bfloat16)

    spec_in = (P(row_axes, None), P(None, 'tp'), P(None, 'tp'), P(None, 'tp'), P('tp', None), P(row_axes, 'tp', None), P(row_axes, 'tp', None), P(row_axes, None, 'tp', None), P(row_axes, None, 'tp', None), P(row_axes))
    return jax.shard_map(device_step, mesh=mesh, in_specs=spec_in, out_specs=P(row_axes, None), check_vma=False)
```

profile of v0, /device:TPU:0, one launch (start us, length us, event | category | flops | bytes accessed | tf_op | source)
XLA Modules:
  0.0 331.5 jit_solution(12087316755040016012)
XLA Ops:
  6.5 12.5 %convolution_convert_fusion = bf16[128,2560]{1,0:T(8,128)(2,1)S(1)} fusion(bf16[128,5120]{1,0:T(8,128)(2,1)} %param.10, bf16[5120,2560]{1,0:T(8,128)(2,1)} %param.11), kind=kOutput, calls=%fused_computation.18 | convolution fusion | flops 3355770880 | bytes 28180480 | tf_op jit(solution)/shard_map/dot_general | solution.py:17
  19.3 1.1 copy.53
  21.5 24.4 %all-gather.2.cloned.1.call-done = bf16[512,4,5,128]{3,0,2,1:T(8,128)(2,1)} async-done(((bf16[128,4,5,128]{3,0,2,1:T(8,128)(2,1)}), bf16[512,4,5,128]{3,0,2,1:T(8,128)(2,1)}) %all-gather.2.cloned.1.call-update) | async-done | bytes 2621456 | tf_op jit(solution)/shard_map/all_gather | solution.py:21
  45.9 3.3 bitcast_reduce_fusion
  49.2 1.9 fusion.5
  51.1 2.4 bitcast_divide_fusion
  53.6 3.0 pad_maximum_fusion
  56.6 10.4 %copy.59 = f32[512,4,5,129]{3,1,2,0:T(4,128)} copy(f32[512,4,5,129]{0,3,2,1:T(8,128)} %pad_maximum_fusion) | data formatting | bytes 10567680 | tf_op jit(solution)/shard_map/concatenate | solution.py:27
  67.0 6.0 %all-to-all-start = ((f32[512,4,5,129]{3,1,2,0:T(4,128)}), f32[512,4,5,129]{3,1,2,0:T(4,128)}, u32[]{:S(2)}, u32[]{:S(2)}) async-start(f32[512,4,5,129]{3,1,2,0:T(4,128)} %copy.59), calls=%async_computation | async-start | bytes 20971520 | tf_op jit(solution)/shard_map/all_to_all | solution.py:28
  73.3 17.3 %fusion.11 = (f32[128,4,5]{2,1,0:T(4,128)S(1)}, f32[128,4,5,256]{3,2,1,0:T(8,128)}) fusion(pred[128,256]{1,0:T(8,128)(4,1)S(1)} %iota_compare_fusion, bf16[128,4,5,128]{3,2,1,0:T(8,128)(2,1)S(1)} %copy.61, bf16[128,256,4,128]{3,2,1,0:T(4,128)(2,1)} %param.17), kind=kOutput, calls=%fused_computation.17 | convolution fusion | flops 169735680 | bytes 36874240 | tf_op jit(solution)/shard_map/bkgd,bskd->bkgs/dot_general | solution.py:34
  90.6 3.4 %convolution_convert_fusion.2 = bf16[128,512]{1,0:T(8,128)(2,1)S(1)} fusion(bf16[128,5120]{1,0:T(8,128)(2,1)S(1)} %copy-done.2, bf16[5120,512]{1,0:T(8,128)(2,1)} %param.12), kind=kOutput, calls=%fused_computation.29 | convolution fusion | flops 671154176 | bytes 6684672 | tf_op jit(solution)/shard_map/dot_general | solution.py:19
  95.1 3.4 %fusion.13 = f32[128,4,5]{2,1,0:T(4,128)S(1)} fusion(f32[128,4,5,256]{3,2,1,0:T(8,128)} %get-tuple-element.15, f32[128,4,5]{2,1,0:T(4,128)S(1)} %copy.64, pred[128,256]{1,0:T(8,128)(4,1)S(1)} %iota_compare_fusion), kind=kLoop, calls=%fused_computation.20 | loop fusion | flops 2618880 | bytes 2674688 | tf_op jit(solution)/shard_map/reduce_sum | solution.py:40
  98.6 3.4 %fusion.21 = f32[128,512]{1,0:T(8,128)S(1)} fusion(bf16[128,5120]{1,0:T(8,128)(2,1)S(1)} %copy-done.2, bf16[5120,512]{1,0:T(8,128)(2,1)} %param.13), kind=kOutput, calls=%fused_computation.28 | convolution fusion | flops 671219712 | bytes 6815744 | tf_op jit(solution)/shard_map/dot_general | solution.py:20
  102.7 85.6 %all-to-all-done = f32[512,4,5,129]{3,1,2,0:T(4,128)} async-done(((f32[512,4,5,129]{3,1,2,0:T(4,128)}), f32[512,4,5,129]{3,1,2,0:T(4,128)}, u32[]{:S(2)}, u32[]{:S(2)}) %all-to-all-start) | async-done | bytes 5283872 | tf_op jit(solution)/shard_map/all_to_all | solution.py:28
  188.3 6.5 %slice_reduce_fusion = (f32[128,4,5]{1,2,0:T(8,128)S(1)}, f32[4,128,4,5,1]{4,2,3,1,0:T(4,128)}) fusion(f32[4,128,4,5,129]{4,2,3,1,0:T(4,128)} %bitcast.6), kind=kLoop, calls=%fused_computation.48 | loop fusion | flops 7680 | bytes 92160 | tf_op jit(solution)/shard_map/reduce_max | solution.py:44
  195.0 4.7 %copy.85 = f32[4,128,4,5,1]{1,0,4,3,2:T(4,128)S(1)} copy(f32[4,128,4,5,1]{4,2,3,1,0:T(4,128)} %get-tuple-element.11) | data formatting | bytes 81920
  199.9 5.8 %slice.9 = f32[4,128,4,5,128]{4,2,3,1,0:T(4,128)} slice(f32[4,128,4,5,129]{4,2,3,1,0:T(4,128)} %bitcast.6), slice={[0:4], [0:128], [0:4], [0:5], [0:128]} | slice | bytes 10485760 | tf_op jit(solution)/shard_map/slice | solution.py:30
  208.2 7.2 %copy.86 = f32[4,128,4,5,128]{1,0,4,3,2:T(4,128)} copy(f32[4,128,4,5,128]{4,2,3,1,0:T(4,128)} %slice.9) | data formatting | bytes 10485760
  215.5 6.1 %multiply_reduce_fusion = f32[128,4,5,128]{0,3,2,1:T(8,128)S(1)} fusion(f32[4,128,4,5,128]{1,0,4,3,2:T(4,128)} %copy.86, f32[4,128,4,5]{1,0,3,2:T(4,128)S(1)} %exponential_bitcast_fusion), kind=kLoop, calls=%fused_computation.12 | loop fusion | flops 2293760 | bytes 6594560 | tf_op jit(solution)/shard_map/reduce_sum | solution.py:47
  221.6 2.0 copy.70
  223.7 16.4 %divide_convert_fusion = bf16[128,4,5,128]{3,2,1,0:T(8,128)(2,1)S(1)} fusion(f32[128,4,5,128]{3,2,1,0:T(8,128)} %copy.70, f32[128,4,5]{2,1,0:T(4,128)} %copy.71, f32[128,4,5]{2,1,0:T(4,128)} %copy.69, f32[128,4,128]{2,1,0:T(4,128)} %reshape.66, f32[128,4,5]{2,1,0:T(4,128)S(1)} %copy.68, f32[128,4,5]{2,1,0:T(4,128)} %copy.66, ...), kind=kOutput, calls=%fused_computation.22 | convolution fusion | flops 172687360 | bytes 38488064 | tf_op jit(solution)/shard_map/bkgs,bskd->bkgd/dot_general | solution.py:41
  240.9 12.0 %fusion.38 = f32[128,5120]{1,0:T(8,128)} fusion(bf16[128,2560]{0,1:T(8,128)(2,1)S(1)} %bitcast.51, bf16[2560,5120]{1,0:T(8,128)(2,1)} %param.14), kind=kOutput, calls=%fused_computation.51 | convolution fusion | flops 3355443200 | bytes 29491200 | tf_op jit(solution)/shard_map/dot_general | solution.py:50
  252.9 68.7 %all-reduce.2.cloned.1.call-done = f32[128,5120]{1,0:T(8,128)} async-done(((f32[128,5120]{1,0:T(8,128)}), f32[128,5120]{1,0:T(8,128)}) %all-reduce.2.cloned.1.call-update) | async-done | bytes 2621456 | tf_op jit(solution)/shard_map/psum | solution.py:51
  321.6 3.1 add_convert_fusion
  (37 shorter events, 7.6 us)
Async XLA Ops:
  6.5 39.3 %copy-start = (bf16[256,4,128]{2,1,0:T(4,128)(2,1)S(1)}, bf16[256,4,128]{2,1,0:T(4,128)(2,1)}, u32[]{:S(2)}) copy-start(bf16[256,4,128]{2,1,0:T(4,128)(2,1)} %param.15) | copy-start | bytes 786436
  6.5 39.3 %all-gather.2.cloned.1.call-start = ((), (), s32[]{:S(2)}) async-start(), calls=%async_computation.1 | async-start | bytes 3276800 | tf_op jit(solution)/shard_map/all_gather | solution.py:21
  19.0 2.4 copy-start.3
  49.2 1.9 copy-start.4
  67.0 121.3 %all-to-all-start = ((f32[512,4,5,129]{3,1,2,0:T(4,128)}), f32[512,4,5,129]{3,1,2,0:T(4,128)}, u32[]{:S(2)}, u32[]{:S(2)}) async-start(f32[512,4,5,129]{3,1,2,0:T(4,128)} %copy.59), calls=%async_computation | async-start | bytes 20971520 | tf_op jit(solution)/shard_map/all_to_all | solution.py:28
  73.0 17.6 %copy-start.2 = (bf16[128,5120]{1,0:T(8,128)(2,1)S(1)}, bf16[128,5120]{1,0:T(8,128)(2,1)}, u32[]{:S(2)}) copy-start(bf16[128,5120]{1,0:T(8,128)(2,1)} %param.10) | copy-start | bytes 3932164
  73.1 248.5 %all-reduce.2.cloned.1.call-start = ((), (), s32[]{:S(2)}) async-start(), calls=%async_computation.2 | async-start | bytes 5242880 | tf_op jit(solution)/shard_map/psum | solution.py:51
  240.9 83.7 %copy-start.1 = (bf16[256,4,128]{2,1,0:T(4,128)(2,1)S(1)}, bf16[256,4,128]{2,1,0:T(4,128)(2,1)}, u32[]{:S(2)}) copy-start(bf16[256,4,128]{2,1,0:T(4,128)(2,1)} %param.15) | copy-start | bytes 786436
Sparse Core Ops, SparseCore 0:
  20.6 25.2 all-gather.1
  253.0 68.5 all-reduce.1
where the time goes:
time: 332 us; the launch traced here: 331 us
  waiting for transfers between devices  179 us (54%)
  matrix products  71.2 us (21%)
  local copies, waits for them, and re-layouts  37.7 us (11%)
  other arithmetic  24.1 us (7%)
  between operations  13.6 us (4%)
  starting transfers between devices  6.21 us (2%)
    all_to_all x1, waiting for transfers between devices, device_step(): returned = lax.all_to_all(partial_state, 'ctx', 0, 0, tiled=True)  85.6 us
    psum x1, waiting for transfers between devices, device_step(): out_hidden = hidden.astype(jnp.float32) + lax.psum(proj_part, 'tp')  68.7 us
    all_gather x1, waiting for transfers between devices, device_step(): q_every = lax.all_gather(q_local, 'ctx', axis=0, tiled=True)  24.4 us
    dot_general x1, matrix products, device_step(): jnp.einsum('bkgd,bskd->bkgs', q_local, k_suffix, preferred_element_type=j...  17.3 us
    dot_general x1, matrix products, device_step(): jnp.einsum('bkgs,bskd->bkgd', e_cache.astype(jnp.bfloat16), v_suffix, pre...  16.4 us
    dot_general x1, matrix products, device_step(): jnp.dot(hidden, w_q, preferred_element_type=jnp.float32)  12.5 us
    unnamed x13, local copies, waits for them, and re-layouts  12.2 us
    dot_general x1, matrix products, device_step(): proj_part = jnp.dot(attn_out, w_o, preferred_element_type=jnp.float32)  12 us
  transfers between devices with their start and end apart: 3, of which 3 were waited for; matrix products, arithmetic and copies ran while one was open for 9% of the time, Pallas kernels for 0%

commit v1 on v0

v1 whole, which is shorter than its diff:
```python
import functools

import jax
import jax.numpy as jnp
from jax import lax
from jax.experimental import pallas as pl
from jax.experimental.pallas import tpu as pltpu
from jax.sharding import PartitionSpec as P

MESH = pl.DeviceIdType.MESH
F32 = jnp.float32
BF16 = jnp.bfloat16
LOG2E = 1.4426950408889634
LOW = -3.0e38

CB = 512
SUB = 32
GRP = 8
RING = 3
PAD = 24


def mm(a, b):
    return jnp.dot(a, b, preferred_element_type=F32)


def mmt(a, b):
    return lax.dot_general(a, b, (((1,), (1,)), ((), ())), preferred_element_type=F32)


def body(dims, hid, wq, wk, wv, wo, kp, vp, ks, vs, lens, out,
         x_v, xo_v, wo_v, k_ring, v_ring, q2, qg, kn, vn, pre, dei, kvp, key,
         o2, m2, l2, att, snd, rcv, own, yo, yp,
         x_sem, p_sem, w_sem, wo_sem, kv_sem, g_snd, g_rcv, f_snd, f_rcv, y_snd, y_rcv, o_sem):
    nseq, model, heads, kvh, hd, slots = dims
    grp_heads = heads // kvh
    rows = slots * kvh
    half = model // 2
    nq = heads * hd // CB
    nh = half // CB
    nsub = nseq // SUB
    ngrp = nseq // GRP
    gps = SUB // GRP
    kdim = heads * hd
    c = lax.axis_index('ctx')
    t = lax.axis_index('tp')
    far = {'ctx': lax.rem(c + 2, 4)}
    near = {'ctx': c + 1 - 2 * lax.rem(c, 2)}
    mate = {'tp': 1 - t}
    cs = LOG2E * hd ** -0.5

    def remote(src, dst, ss, rs, dev):
        return pltpu.make_async_remote_copy(src_ref=src, dst_ref=dst, send_sem=ss, recv_sem=rs,
                                            device_id=dev, device_id_type=MESH)

    def w_copies(src, col, slot):
        return [pltpu.make_async_copy(src.at[pl.ds(i * kdim, kdim), pl.ds(col, CB)],
                                      wo_v.at[2 * slot + i], w_sem.at[slot, i]) for i in range(2)]

    def w_start(src, col, slot):
        for cp in w_copies(src, col, slot):
            cp.start()

    def wo_copy(j):
        col = jnp.where(j < nh, (1 - t) * half, t * half - half) + j * CB
        return pltpu.make_async_copy(wo.at[:, pl.ds(pl.multiple_of(col, CB), CB)], wo_v.at[j], wo_sem.at[j])

    def kv_copies(g):
        slot = lax.rem(g, RING)
        src = pl.ds(g * GRP * rows, GRP * rows)
        return [pltpu.make_async_copy(ks.at[src], k_ring.at[slot], kv_sem.at[slot, 0]),
                pltpu.make_async_copy(vs.at[src], v_ring.at[slot], kv_sem.at[slot, 1])]

    def kv_start(g):
        for cp in kv_copies(g):
            cp.start()

    x_copy = pltpu.make_async_copy(hid, x_v, x_sem.at[0])
    xo_copy = pltpu.make_async_copy(hid.at[:, pl.ds(pl.multiple_of(t * half, CB), half)], xo_v, x_sem.at[1])
    p_copies = [pltpu.make_async_copy(kp, pre.at[0], p_sem.at[0]), pltpu.make_async_copy(vp, pre.at[1], p_sem.at[1])]
    p_copies[0].start()
    p_copies[1].start()
    x_copy.start()
    for n in range(RING):
        w_start(wq, n * CB, n)
    xo_copy.start()

    barrier = pltpu.get_barrier_semaphore()
    for dev in (far, near, mate):
        pl.semaphore_signal(barrier, inc=1, device_id=dev, device_id_type=MESH)

    for i in range(2):
        p_copies[i].wait()
        dei[...] = pre[i].astype(F32)
        for h in range(kvh):
            kvp[0, i, h] = dei[pl.ds(h, kvp.shape[3], stride=kvh), :].astype(BF16)
    pl.semaphore_wait(barrier, 3)
    to_far = remote(kvp.at[0], kvp.at[2], g_snd.at[0], g_rcv.at[0], far)
    to_near = remote(kvp.at[0], kvp.at[1], g_snd.at[1], g_rcv.at[1], near)
    pass_on = remote(kvp.at[2], kvp.at[3], g_snd.at[2], g_rcv.at[2], near)
    to_far.start()
    to_near.start()

    row_head = lax.broadcasted_iota(jnp.int32, (PAD, rows), 0) // grp_heads
    col_row = lax.broadcasted_iota(jnp.int32, (PAD, rows), 1)
    key[...] = jnp.where(lax.rem(col_row, kvh) == row_head, col_row // kvh, slots)
    for h in range(heads, PAD):
        q2[pl.ds(h, nseq, stride=PAD), :] = jnp.zeros((nseq, hd), F32)

    x_copy.wait()

    def project(slot):
        return mm(x_v[:, :kdim], wo_v[2 * slot]) + mm(x_v[:, kdim:], wo_v[2 * slot + 1])

    hpb = CB // hd

    def q_block(n, carry):
        slot = lax.rem(n, RING)
        for cp in w_copies(wq, pl.multiple_of(n * CB, CB), slot):
            cp.wait()
        q = project(slot).astype(BF16)
        for i in range(hpb):
            one = q[:, i * hd:(i + 1) * hd]
            qg[hpb * n + i] = one
            q2[pl.ds(hpb * n + i, nseq, stride=PAD), :] = one.astype(F32)

        @pl.when(n + RING < nq)
        def _():
            w_start(wq, pl.multiple_of((n + RING) * CB, CB), slot)

        @pl.when(n + RING == nq)
        def _():
            w_start(wk, 0, slot)

        @pl.when(n + RING == nq + 1)
        def _():
            w_start(wv, 0, slot)
            kv_start(0)

        @pl.when(n + RING == nq + 2)
        def _():
            kv_start(1)
        return carry

    lax.fori_loop(0, nq, q_block, 0)
    for n, src, dst in ((nq, wk, kn), (nq + 1, wv, vn)):
        for cp in w_copies(src, 0, n % RING):
            cp.wait()
        new = project(n % RING).astype(BF16).astype(F32)
        for h in range(kvh):
            dst[h] = new[:, h * hd:(h + 1) * hd]
        if n == nq:
            kv_start(2)
    xo_copy.wait()

    zero8 = jnp.zeros((8, hd), F32)
    zero32 = jnp.zeros((32, hd), BF16)
    quarter = rows // 4

    def attend(g):
        slot = lax.rem(g, RING)
        for i in range(GRP):
            b = g * GRP + i
            q = q2[pl.ds(pl.multiple_of(b * PAD, 8), PAD), :]
            q = jnp.concatenate([q, zero8], 0).astype(BF16)
            lhs = jnp.concatenate([jnp.concatenate([q, zero32], 1), jnp.concatenate([zero32, q], 1)], 0)
            base = i * rows
            s = []
            for p in range(2):
                k0 = k_ring[slot, base + 2 * p * quarter:base + (2 * p + 1) * quarter, :]
                k1 = k_ring[slot, base + (2 * p + 1) * quarter:base + (2 * p + 2) * quarter, :]
                r = mmt(lhs, jnp.concatenate([k0, k1], 1))
                s += [r[0:PAD], r[32:32 + PAD]]
            n_old = lens[b]
            s = [jnp.where(key[:, p * quarter:(p + 1) * quarter] < n_old, s[p], -jnp.inf) for p in range(4)]
            m = jnp.maximum(jnp.maximum(s[0], s[1]), jnp.maximum(s[2], s[3]))
            m = jnp.maximum(jnp.max(m, axis=1, keepdims=True), LOW)
            e = [jnp.exp2((a - m) * cs) for a in s]
            l = jnp.sum((e[0] + e[1]) + (e[2] + e[3]), axis=1, keepdims=True)
            gap = jnp.zeros((8, 2 * quarter), F32)
            w = jnp.concatenate([jnp.concatenate([e[0], e[2]], 1), gap,
                                 jnp.concatenate([e[1], e[3]], 1), gap], 0).astype(BF16)
            v = [v_ring[slot, base + p * quarter:base + (p + 1) * quarter, :] for p in range(4)]
            v = jnp.concatenate([jnp.concatenate([v[0], v[1]], 1), jnp.concatenate([v[2], v[3]], 1)], 0)
            o = mm(w, v)
            at = pl.ds(pl.multiple_of(lax.rem(b, SUB) * PAD, 8), PAD)
            o2[at, :] = o[0:PAD, :hd] + o[32:32 + PAD, hd:]
            m2[at, :] = jnp.broadcast_to(m, (PAD, hd))
            l2[at, :] = jnp.broadcast_to(l, (PAD, hd))

    def group(g, carry):
        for cp in kv_copies(g):
            cp.wait()
        attend(g)

        @pl.when(jnp.logical_or(g == 0, jnp.logical_and(g >= gps, g + RING < ngrp)))
        def _():
            kv_start(g + RING)

        wo_steps = [(0, 2), (2, 5), (5, 8), (8, 2 * nh)]
        for n, (lo, hi) in enumerate(wo_steps):
            @pl.when(g == n)
            def _():
                for j in range(lo, hi):
                    wo_copy(j).start()

        @pl.when(g == gps - 1)
        def _():
            for n in range(gps, gps + RING):
                kv_start(n)

        @pl.when(g == 1)
        def _():
            to_far.wait_recv()
            pass_on.start()
        return carry

    def merge(s, h):
        at = pl.ds(pl.multiple_of(s * SUB, SUB), SUB)
        q = qg[pl.ds(h * grp_heads, grp_heads), at, :].reshape(grp_heads * SUB, hd)
        sc = [mmt(q, kvp[n, 0, h]) for n in range(4)]
        m = jnp.maximum(jnp.maximum(sc[0], sc[1]), jnp.maximum(sc[2], sc[3]))
        m = jnp.max(m, axis=1, keepdims=True)
        e = [jnp.exp2((a - m) * cs) for a in sc]
        l = jnp.sum((e[0] + e[1]) + (e[2] + e[3]), axis=1, keepdims=True)
        o = mm(jnp.concatenate([a.astype(BF16) for a in e], 1),
               jnp.concatenate([kvp[n, 1, h] for n in range(4)], 0))
        k_new = kn[h, at, :]
        v_new = vn[h, at, :]
        for i in range(grp_heads):
            part = slice(i * SUB, (i + 1) * SUB)
            rows_at = pl.ds(h * grp_heads + i, SUB, stride=PAD)
            m_s, l_s, o_s = m2[rows_at, :], l2[rows_at, :], o2[rows_at, :]
            s_n = jnp.sum(q[part].astype(F32) * k_new, axis=1, keepdims=True)
            m_p = jnp.maximum(m[part], s_n)
            m_all = jnp.maximum(m_p, m_s)
            w_p = jnp.exp2((m[part] - m_all) * cs)
            w_n = jnp.exp2((s_n - m_all) * cs)
            w_s = jnp.exp2((m_s - m_all) * cs)
            total = w_p * l[part] + w_n + w_s * l_s
            val = (w_p * o[part] + w_n * v_new + w_s * o_s) / total
            att[h * grp_heads + i] = val.astype(BF16)

    def a_rows():
        return jnp.concatenate([att[h] for h in range(heads)], 1)

    def partial_copy(s, j):
        return remote(snd.at[s, j], rcv.at[s, j], f_snd.at[s, j], f_rcv.at[s, j], mate)

    def y_copy(s, j):
        return remote(yo.at[s, j], yp.at[s, j], y_snd.at[s, j], y_rcv.at[s, j], mate)

    def out_copy(src, which, s, j):
        side = t if which == 0 else 1 - t
        col = pl.multiple_of(side * half + j * CB, CB)
        return pltpu.make_async_copy(src.at[s, j], out.at[pl.ds(pl.multiple_of(s * SUB, SUB), SUB), pl.ds(col, CB)],
                                     o_sem.at[which, s, j])

    def finish(s):
        def step(j, carry):
            partial_copy(s, j).wait_recv()
            yo[s, j] = (own[s, j] + rcv[s, j]).astype(BF16)
            y_copy(s, j).start()
            out_copy(yo, 0, s, j).start()
            return carry
        lax.fori_loop(0, nh, step, 0)

    def sub_pass(s, carry):
        lax.fori_loop(s * gps, (s + 1) * gps, group, 0)

        @pl.when(s == 0)
        def _():
            to_near.wait_recv()
            pass_on.wait_recv()

        def one_head(h, cc):
            merge(s, h)
            return cc
        lax.fori_loop(0, kvh, one_head, 0)

        def send(j, cc):
            @pl.when(s == 0)
            def _():
                wo_copy(j).wait()
            snd[s, j] = mm(a_rows(), wo_v[j])
            partial_copy(s, j).start()
            return cc
        lax.fori_loop(0, nh, send, 0)

        def keep(j, cc):
            @pl.when(s == 0)
            def _():
                wo_copy(nh + j).wait()
            x_at = xo_v[pl.ds(pl.multiple_of(s * SUB, SUB), SUB), pl.ds(pl.multiple_of(j * CB, CB), CB)]
            own[s, j] = mm(a_rows(), wo_v[nh + j]) + x_at.astype(F32)
            return cc
        lax.fori_loop(0, nh, keep, 0)

        @pl.when(s > 0)
        def _():
            finish(s - 1)
        return carry

    lax.fori_loop(0, nsub, sub_pass, 0)
    finish(nsub - 1)

    def tail(n, carry):
        s, j = n // nh, lax.rem(n, nh)
        y_copy(s, j).wait_recv()
        out_copy(yp, 1, s, j).start()
        return carry
    lax.fori_loop(0, nsub * nh, tail, 0)

    def drain(n, carry):
        s, j = n // nh, lax.rem(n, nh)
        partial_copy(s, j).wait_send()
        y_copy(s, j).wait_send()
        out_copy(yo, 0, s, j).wait()
        out_copy(yp, 1, s, j).wait()
        return carry
    lax.fori_loop(0, nsub * nh, drain, 0)
    to_far.wait_send()
    to_near.wait_send()
    pass_on.wait_send()


def solution(mesh):
    row_axes = ('dp', 'ctx')

    def device_step(hidden, w_q, w_k, w_v, w_o, k_prefix, v_prefix, k_suffix, v_suffix, seq_lens):
        nseq, model = hidden.shape
        npos, kvh, hd = k_prefix.shape
        slots = k_suffix.shape[1]
        heads = w_q.shape[1] // hd
        rows = slots * kvh
        nsub, nh = nseq // SUB, model // 2 // CB
        dims = (nseq, model, heads, kvh, hd, slots)
        hbm = pl.BlockSpec(memory_space=pl.ANY)
        dma = pltpu.SemaphoreType.DMA
        return pl.pallas_call(
            functools.partial(body, dims),
            out_shape=jax.ShapeDtypeStruct((nseq, model), BF16),
            in_specs=[hbm] * 9 + [pl.BlockSpec(memory_space=pltpu.SMEM)],
            out_specs=hbm,
            scratch_shapes=[
                pltpu.VMEM((nseq, model), BF16),
                pltpu.VMEM((nseq, model // 2), BF16),
                pltpu.VMEM((2 * nh, heads * hd, CB), BF16),
                pltpu.VMEM((RING, GRP * rows, hd), BF16),
                pltpu.VMEM((RING, GRP * rows, hd), BF16),
                pltpu.VMEM((nseq * PAD, hd), F32),
                pltpu.VMEM((heads, nseq, hd), BF16),
                pltpu.VMEM((kvh, nseq, hd), F32),
                pltpu.VMEM((kvh, nseq, hd), F32),
                pltpu.VMEM((2, npos * kvh, hd), BF16),
                pltpu.VMEM((npos * kvh, hd), F32),
                pltpu.VMEM((4, 2, kvh, npos, hd), BF16),
                pltpu.VMEM((PAD, rows), jnp.int32),
                pltpu.VMEM((SUB * PAD, hd), F32),
                pltpu.VMEM((SUB * PAD, hd), F32),
                pltpu.VMEM((SUB * PAD, hd), F32),
                pltpu.VMEM((heads, SUB, hd), BF16),
                pltpu.VMEM((nsub, nh, SUB, CB), F32),
                pltpu.VMEM((nsub, nh, SUB, CB), F32),
                pltpu.VMEM((nsub, nh, SUB, CB), F32),
                pltpu.VMEM((nsub, nh, SUB, CB), BF16),
                pltpu.VMEM((nsub, nh, SUB, CB), BF16),
                dma((2,)), dma((2,)), dma((RING, 2)), dma((2 * nh,)), dma((RING, 2)),
                dma((3,)), dma((3,)), dma((nsub, nh)), dma((nsub, nh)), dma((nsub, nh)), dma((nsub, nh)),
                dma((2, nsub, nh)),
            ],
            compiler_params=pltpu.CompilerParams(collective_id=0, has_side_effects=True,
                                                 vmem_limit_bytes=67043328),
        )(hidden, w_q, w_k, w_v, w_o,
          k_prefix.reshape(npos * kvh, hd), v_prefix.reshape(npos * kvh, hd),
          k_suffix.reshape(nseq * rows, hd), v_suffix.reshape(nseq * rows, hd), seq_lens)

    spec_in = (P(row_axes, None), P(None, 'tp'), P(None, 'tp'), P(None, 'tp'), P('tp', None), P(row_axes, 'tp', None), P(row_axes, 'tp', None), P(row_axes, None, 'tp', None), P(row_axes, None, 'tp', None), P(row_axes))
    return jax.shard_map(device_step, mesh=mesh, in_specs=spec_in, out_specs=P(row_axes, None), check_vma=False)
```

time: 332 us -> 109 us (0.33)
  waiting for transfers between devices: 179 us -> 0 us
  Pallas kernels: 0 us -> 106 us
  matrix products: 71.2 us -> 0 us
  local copies, waits for them, and re-layouts: 37.7 us -> 2.46 us
  other arithmetic: 24.1 us -> 0 us
  between operations: 13.6 us -> 0.01 us
  starting transfers between devices: 6.21 us -> 0 us
    pallas_call x0 -> x1, Pallas kernels: none -> 106 us  [device_step(): pl.pallas_call(functools.partial(body, dims), out_shape=jax.ShapeDtypeStr...]
    all_to_all x1 -> x0, waiting for transfers between devices: 85.6 us -> none  [device_step(): returned = lax.all_to_all(partial_state, 'ctx', 0, 0, tiled=True)]
    dot_general x9 -> x0, matrix products: 71.2 us -> none  [the longest x1 17.3 us: device_step(): jnp.einsum('bkgd,bskd->bkgs', q_local, k_suffix, preferred_element_type=j...]
    psum x1 -> x0, waiting for transfers between devices: 68.7 us -> none  [device_step(): out_hidden = hidden.astype(jnp.float32) + lax.psum(proj_part, 'tp')]
    all_gather x1 -> x0, waiting for transfers between devices: 24.4 us -> none  [device_step(): q_every = lax.all_gather(q_local, 'ctx', axis=0, tiled=True)]
    reduce_sum x4 -> x0, other arithmetic: 11.4 us -> none  [the longest x1 6.07 us: device_step(): jnp.sum(w_parts[..., None] * o_parts, axis=0) + w_suf[..., None] * o_suf]
    concatenate x1 -> x0, local copies, waits for them, and re-layouts: 10.4 us -> none  [device_step(): jnp.concatenate([o_pre / l_pre[..., None], (m_pre + jnp.log(l_pre))[...,...]
    unnamed x13 -> x1, local copies, waits for them, and re-layouts: 12.2 us -> 2.46 us
  transfers between devices with their start and end apart: 3 -> 0, of which waited for: 3 -> 0; matrix products, arithmetic and copies ran while one was open for 9% -> 0% of each run, Pallas kernels for 0% -> 0%
where the time goes in v1:
time: 109 us
  Pallas kernels  106 us (97%)
  local copies, waits for them, and re-layouts  2.46 us (2%)
    pallas_call x1, Pallas kernels, device_step(): pl.pallas_call(functools.partial(body, dims), out_shape=jax.ShapeDtypeStr...  106 us
    unnamed x1, local copies, waits for them, and re-layouts  2.46 us

profile of v1, /device:TPU:0, one launch (start us, length us, event | category | flops | bytes accessed | tf_op | source)
XLA Modules:
  0.0 108.6 jit_solution(928979822132875539)
XLA Ops:
  0.0 106.2 %shard_map.100 = bf16[128,5120]{1,0:T(8,128)(2,1)} custom-call(bf16[128,5120]{1,0:T(8,128)(2,1)} %hid.1, bf16[5120,2560]{1,0:T(8,128)(2,1)} %wq.1, bf16[5120,512]{1,0:T(8,128)(2,1)} %wk.1, bf16[5120,512]{1,0:T(8,128)(2,1)} %wv.1, bf16[2560,5120]{1,0:T(8,128)(2,1)} %wo.1, bf16[1024,128]{1,0:T(8,128)(2,1)} %bitcast.6, bf16[1024,128]{1,0:T(8,128)(2,1)} %bitcast.7, ...), custom_call_target="tpu_custom_call" | custom-call | tf_op jit(solution)/shard_map/pallas_call | solution.py:340
  106.2 2.5 %copy.12 = bf16[128,5120]{1,0:T(8,128)(2,1)} copy(bf16[128,5120]{1,0:T(8,128)(2,1)} %shard_map.100) | data formatting | bytes 2621440

commit v2 on v1

--- a/solution.py
+++ b/solution.py
@@ -157,36 +157,50 @@
     zero32 = jnp.zeros((32, hd), BF16)
     quarter = rows // 4
 
+    def scores(slot, b, base):
+        q = q2[pl.ds(pl.multiple_of(b * PAD, 8), PAD), :]
+        q = jnp.concatenate([q, zero8], 0).astype(BF16)
+        lhs = jnp.concatenate([jnp.concatenate([q, zero32], 1), jnp.concatenate([zero32, q], 1)], 0)
+        s = []
+        for p in range(2):
+            k0 = k_ring[slot, base + 2 * p * quarter:base + (2 * p + 1) * quarter, :]
+            k1 = k_ring[slot, base + (2 * p + 1) * quarter:base + (2 * p + 2) * quarter, :]
+            r = mmt(lhs, jnp.concatenate([k0, k1], 1))
+            s += [r[0:PAD], r[32:32 + PAD]]
+        return s
+
+    def weights(s, b):
+        n_old = lens[b]
+        s = [jnp.where(key[:, p * quarter:(p + 1) * quarter] < n_old, s[p], -jnp.inf) for p in range(4)]
+        m = jnp.maximum(jnp.maximum(s[0], s[1]), jnp.maximum(s[2], s[3]))
+        m = jnp.maximum(jnp.max(m, axis=1, keepdims=True), LOW)
+        e = [jnp.exp2((a - m) * cs) for a in s]
+        l = jnp.sum((e[0] + e[1]) + (e[2] + e[3]), axis=1, keepdims=True)
+        gap = jnp.zeros((8, 2 * quarter), F32)
+        w = jnp.concatenate([jnp.concatenate([e[0], e[2]], 1), gap,
+                             jnp.concatenate([e[1], e[3]], 1), gap], 0).astype(BF16)
+        at = pl.ds(pl.multiple_of(lax.rem(b, SUB) * PAD, 8), PAD)
+        m2[at, :] = jnp.broadcast_to(m, (PAD, hd))
+        l2[at, :] = jnp.broadcast_to(l, (PAD, hd))
+        return w
+
+    def values(w, slot, b, base):
+        v = [v_ring[slot, base + p * quarter:base + (p + 1) * quarter, :] for p in range(4)]
+        v = jnp.concatenate([jnp.concatenate([v[0], v[1]], 1), jnp.concatenate([v[2], v[3]], 1)], 0)
+        o = mm(w, v)
+        at = pl.ds(pl.multiple_of(lax.rem(b, SUB) * PAD, 8), PAD)
+        o2[at, :] = o[0:PAD, :hd] + o[32:32 + PAD, hd:]
+
     def attend(g):
         slot = lax.rem(g, RING)
-        for i in range(GRP):
-            b = g * GRP + i
-            q = q2[pl.ds(pl.multiple_of(b * PAD, 8), PAD), :]
-            q = jnp.concatenate([q, zero8], 0).astype(BF16)
-            lhs = jnp.concatenate([jnp.concatenate([q, zero32], 1), jnp.concatenate([zero32, q], 1)], 0)
-            base = i * rows
-            s = []
-            for p in range(2):
-                k0 = k_ring[slot, base + 2 * p * quarter:base + (2 * p + 1) * quarter, :]
-                k1 = k_ring[slot, base + (2 * p + 1) * quarter:base + (2 * p + 2) * quarter, :]
-                r = mmt(lhs, jnp.concatenate([k0, k1], 1))
-                s += [r[0:PAD], r[32:32 + PAD]]
-            n_old = lens[b]
-            s = [jnp.where(key[:, p * quarter:(p + 1) * quarter] < n_old, s[p], -jnp.inf) for p in range(4)]
-            m = jnp.maximum(jnp.maximum(s[0], s[1]), jnp.maximum(s[2], s[3]))
-            m = jnp.maximum(jnp.max(m, axis=1, keepdims=True), LOW)
-            e = [jnp.exp2((a - m) * cs) for a in s]
-            l = jnp.sum((e[0] + e[1]) + (e[2] + e[3]), axis=1, keepdims=True)
-            gap = jnp.zeros((8, 2 * quarter), F32)
-            w = jnp.concatenate([jnp.concatenate([e[0], e[2]], 1), gap,
-                                 jnp.concatenate([e[1], e[3]], 1), gap], 0).astype(BF16)
-            v = [v_ring[slot, base + p * quarter:base + (p + 1) * quarter, :] for p in range(4)]
-            v = jnp.concatenate([jnp.concatenate([v[0], v[1]], 1), jnp.concatenate([v[2], v[3]], 1)], 0)
-            o = mm(w, v)
-            at = pl.ds(pl.multiple_of(lax.rem(b, SUB) * PAD, 8), PAD)
-            o2[at, :] = o[0:PAD, :hd] + o[32:32 + PAD, hd:]
-            m2[at, :] = jnp.broadcast_to(m, (PAD, hd))
-            l2[at, :] = jnp.broadcast_to(l, (PAD, hd))
+        s, w = {}, {}
+        for n in range(GRP + 2):
+            if n < GRP:
+                s[n] = scores(slot, g * GRP + n, n * rows)
+            if 0 <= n - 2 < GRP:
+                values(w.pop(n - 2), slot, g * GRP + n - 2, (n - 2) * rows)
+            if 0 <= n - 1 < GRP:
+                w[n - 1] = weights(s.pop(n - 1), g * GRP + n - 1)
 
     def group(g, carry):
         for cp in kv_copies(g):
@@ -215,31 +229,47 @@
             pass_on.start()
         return carry
 
-    def merge(s, h):
+    def merge(s):
         at = pl.ds(pl.multiple_of(s * SUB, SUB), SUB)
-        q = qg[pl.ds(h * grp_heads, grp_heads), at, :].reshape(grp_heads * SUB, hd)
-        sc = [mmt(q, kvp[n, 0, h]) for n in range(4)]
-        m = jnp.maximum(jnp.maximum(sc[0], sc[1]), jnp.maximum(sc[2], sc[3]))
-        m = jnp.max(m, axis=1, keepdims=True)
-        e = [jnp.exp2((a - m) * cs) for a in sc]
-        l = jnp.sum((e[0] + e[1]) + (e[2] + e[3]), axis=1, keepdims=True)
-        o = mm(jnp.concatenate([a.astype(BF16) for a in e], 1),
-               jnp.concatenate([kvp[n, 1, h] for n in range(4)], 0))
-        k_new = kn[h, at, :]
-        v_new = vn[h, at, :]
-        for i in range(grp_heads):
-            part = slice(i * SUB, (i + 1) * SUB)
-            rows_at = pl.ds(h * grp_heads + i, SUB, stride=PAD)
-            m_s, l_s, o_s = m2[rows_at, :], l2[rows_at, :], o2[rows_at, :]
-            s_n = jnp.sum(q[part].astype(F32) * k_new, axis=1, keepdims=True)
-            m_p = jnp.maximum(m[part], s_n)
-            m_all = jnp.maximum(m_p, m_s)
-            w_p = jnp.exp2((m[part] - m_all) * cs)
-            w_n = jnp.exp2((s_n - m_all) * cs)
-            w_s = jnp.exp2((m_s - m_all) * cs)
-            total = w_p * l[part] + w_n + w_s * l_s
-            val = (w_p * o[part] + w_n * v_new + w_s * o_s) / total
-            att[h * grp_heads + i] = val.astype(BF16)
+
+        def pre_scores(h):
+            q = qg[h * grp_heads:(h + 1) * grp_heads, at, :].reshape(grp_heads * SUB, hd)
+            return q, [mmt(q, kvp[n, 0, h]) for n in range(4)]
+
+        def pre_weights(sc):
+            m = jnp.maximum(jnp.maximum(sc[0], sc[1]), jnp.maximum(sc[2], sc[3]))
+            m = jnp.max(m, axis=1, keepdims=True)
+            e = [jnp.exp2((a - m) * cs) for a in sc]
+            l = jnp.sum((e[0] + e[1]) + (e[2] + e[3]), axis=1, keepdims=True)
+            return jnp.concatenate([a.astype(BF16) for a in e], 1), m, l
+
+        def join(h, q, w, m, l):
+            o = mm(w, jnp.concatenate([kvp[n, 1, h] for n in range(4)], 0))
+            k_new = kn[h, at, :]
+            v_new = vn[h, at, :]
+            for i in range(grp_heads):
+                part = slice(i * SUB, (i + 1) * SUB)
+                rows_at = pl.ds(h * grp_heads + i, SUB, stride=PAD)
+                m_s, l_s, o_s = m2[rows_at, :], l2[rows_at, :], o2[rows_at, :]
+                s_n = jnp.sum(q[part].astype(F32) * k_new, axis=1, keepdims=True)
+                m_p = jnp.maximum(m[part], s_n)
+                m_all = jnp.maximum(m_p, m_s)
+                w_p = jnp.exp2((m[part] - m_all) * cs)
+                w_n = jnp.exp2((s_n - m_all) * cs)
+                w_s = jnp.exp2((m_s - m_all) * cs)
+                total = w_p * l[part] + w_n + w_s * l_s
+                val = (w_p * o[part] + w_n * v_new + w_s * o_s) / total
+                att[h * grp_heads + i] = val.astype(BF16)
+
+        sc, w = {}, {}
+        for n in range(kvh + 2):
+            if n < kvh:
+                sc[n] = pre_scores(n)
+            if 0 <= n - 2 < kvh:
+                join(n - 2, *w.pop(n - 2))
+            if 0 <= n - 1 < kvh:
+                q, p = sc.pop(n - 1)
+                w[n - 1] = (q,) + pre_weights(p)
 
     def a_rows():
         return jnp.concatenate([att[h] for h in range(heads)], 1)
@@ -273,10 +303,7 @@
             to_near.wait_recv()
             pass_on.wait_recv()
 
-        def one_head(h, cc):
-            merge(s, h)
-            return cc
-        lax.fori_loop(0, kvh, one_head, 0)
+        merge(s)
 
         def send(j, cc):
             @pl.when(s == 0)

time: 109 us -> 85.4 us (0.78)
  Pallas kernels: 106 us -> 82.8 us
    pallas_call x1, Pallas kernels: 106 us -> 82.8 us  [device_step(): pl.pallas_call(functools.partial(body, dims), out_shape=jax.ShapeDtypeStr...]
where the time goes in v2:
time: 85.4 us; the launch traced here: 85.3 us
  Pallas kernels  82.8 us (97%)
  local copies, waits for them, and re-layouts  2.46 us (3%)
    pallas_call x1, Pallas kernels, device_step(): pl.pallas_call(functools.partial(body, dims), out_shape=jax.ShapeDtypeStr...  82.8 us
    unnamed x1, local copies, waits for them, and re-layouts  2.46 us

profile of v2, /device:TPU:0, one launch (start us, length us, event | category | flops | bytes accessed | tf_op | source)
XLA Modules:
  0.0 85.3 jit_solution(14900323109417442242)
XLA Ops:
  0.0 82.8 %shard_map.100 = bf16[128,5120]{1,0:T(8,128)(2,1)} custom-call(bf16[128,5120]{1,0:T(8,128)(2,1)} %hid.1, bf16[5120,2560]{1,0:T(8,128)(2,1)} %wq.1, bf16[5120,512]{1,0:T(8,128)(2,1)} %wk.1, bf16[5120,512]{1,0:T(8,128)(2,1)} %wv.1, bf16[2560,5120]{1,0:T(8,128)(2,1)} %wo.1, bf16[1024,128]{1,0:T(8,128)(2,1)} %bitcast.6, bf16[1024,128]{1,0:T(8,128)(2,1)} %bitcast.7, ...), custom_call_target="tpu_custom_call" | custom-call | tf_op jit(solution)/shard_map/pallas_call | solution.py:367
  82.8 2.5 %copy.12 = bf16[128,5120]{1,0:T(8,128)(2,1)} copy(bf16[128,5120]{1,0:T(8,128)(2,1)} %shard_map.100) | data formatting | bytes 2621440

commit v3 on v2

v3 whole, which is shorter than its diff:
```python
import functools

import jax
import jax.numpy as jnp
from jax import lax
from jax.experimental import pallas as pl
from jax.experimental.pallas import tpu as pltpu
from jax.sharding import PartitionSpec as P

MESH = pl.DeviceIdType.MESH
F32 = jnp.float32
BF16 = jnp.bfloat16
LOG2E = 1.4426950408889634
LOW = -3.0e38

CB = 256
SUB = 32
GRP = 8
RING = 4
AHEAD = 4
WSLOT = 5
PAD = 24


def mm(a, b):
    return jnp.dot(a, b, preferred_element_type=F32)


def mmt(a, b):
    return lax.dot_general(a, b, (((1,), (1,)), ((), ())), preferred_element_type=F32)


def body(dims, hid, wq, wk, wv, wo, kp, vp, ks, vs, lens, out,
         x_v, w_v, wo_v, k_ring, v_ring, q2, qg, qs, kvn, kvs, dei, kvp, key,
         o2, m2, l2, att, snd, rcv, own, ybuf,
         x_sem, p_sem, w_sem, wo_sem, kv_sem, g_snd, g_rcv, q_snd, q_rcv, a_snd, a_rcv,
         f_snd, f_rcv, y_snd, y_rcv):
    nseq, model, heads, kvh, hd, slots = dims
    grp_heads = heads // kvh
    rows = slots * kvh
    half = model // 2
    quart = half // 2
    nq = heads * hd // 2 // CB
    nw = nq + 2
    nh = quart // CB
    nsub = nseq // SUB
    ngrp = nseq // GRP
    gps = SUB // GRP
    npos = kvp.shape[3]
    c = lax.axis_index('ctx')
    t = lax.axis_index('tp')
    core = lax.rem(c, 2)
    sib = c + 1 - 2 * core
    far = {'ctx': lax.rem(c + 2, 4)}
    near = {'ctx': sib}
    mate = {'tp': 1 - t}
    diag = {'tp': 1 - t, 'ctx': sib}
    cs = LOG2E * hd ** -0.5

    def remote(src, dst, ss, rs, dev):
        return pltpu.make_async_remote_copy(src_ref=src, dst_ref=dst, send_sem=ss, recv_sem=rs,
                                            device_id=dev, device_id_type=MESH)

    def w_copy(n):
        if n < nq:
            src, col = wq, core * (nq * CB) + n * CB
        else:
            src, col = (wk, wv)[n - nq], core * CB
        return pltpu.make_async_copy(src.at[:, pl.ds(pl.multiple_of(col, CB), CB)], w_v.at[n % WSLOT], w_sem.at[n])

    def wo_copy(j):
        side = (1 - t) if j < nh else t
        col = side * half + core * quart + (j % nh) * CB
        return pltpu.make_async_copy(wo.at[:, pl.ds(pl.multiple_of(col, CB), CB)],
                                     wo_v.at[j // 2, :, pl.ds(j % 2 * CB, CB)], wo_sem.at[j])

    def kv_copies(g):
        slot = lax.rem(g, RING)
        src = pl.ds(g * GRP * rows, GRP * rows)
        return [pltpu.make_async_copy(ks.at[src], k_ring.at[slot], kv_sem.at[slot, 0]),
                pltpu.make_async_copy(vs.at[src], v_ring.at[slot], kv_sem.at[slot, 1])]

    def kv_start(g):
        for cp in kv_copies(g):
            cp.start()

    pre = [k_ring.at[RING - 1, pl.ds(0, npos * kvh)], v_ring.at[RING - 1, pl.ds(0, npos * kvh)]]
    x_copy = pltpu.make_async_copy(hid, x_v.at[pl.ds(0, nseq)], x_sem.at[0])
    p_copies = [pltpu.make_async_copy(kp, pre[0], p_sem.at[0]), pltpu.make_async_copy(vp, pre[1], p_sem.at[1])]

    barrier = pltpu.get_barrier_semaphore()
    for dev in (near, far, mate, diag):
        pl.semaphore_signal(barrier, inc=1, device_id=dev, device_id_type=MESH)
    p_copies[0].start()
    p_copies[1].start()
    x_copy.start()
    for n in range(AHEAD):
        w_copy(n).start()

    row_head = lax.broadcasted_iota(jnp.int32, (PAD, rows), 0) // grp_heads
    col_row = lax.broadcasted_iota(jnp.int32, (PAD, rows), 1)
    key[...] = jnp.where(lax.rem(col_row, kvh) == row_head, col_row // kvh, slots)
    for h in range(heads, PAD):
        q2[pl.ds(h, nseq, stride=PAD), :] = jnp.zeros((nseq, hd), F32)

    pl.semaphore_wait(barrier, 4)
    x_send = remote(hid, x_v.at[pl.ds(nseq, nseq)], x_sem.at[1], x_sem.at[2], near)
    x_send.start()
    for i in range(2):
        p_copies[i].wait()
        dei[...] = pre[i][...].astype(F32)
        for h in range(kvh):
            kvp[0, i, h] = dei[pl.ds(h, npos, stride=kvh), :].astype(BF16)
    to_far = remote(kvp.at[0], kvp.at[2], g_snd.at[0], g_rcv.at[0], far)
    to_near = remote(kvp.at[0], kvp.at[1], g_snd.at[1], g_rcv.at[1], near)
    pass_on = remote(kvp.at[2], kvp.at[3], g_snd.at[2], g_rcv.at[2], near)
    to_far.start()

    hpb = CB // hd
    mine = core * (nq * hpb)
    theirs = (1 - core) * (nq * hpb)

    def q_copy(n):
        at = pl.ds(hpb * n, hpb)
        return remote(qs.at[at], qg.at[pl.ds(mine + hpb * n, hpb)], q_snd.at[n], q_rcv.at[n], near)

    def kv_new_copy(i):
        return remote(kvs.at[i], kvn.at[i, pl.ds(core * hpb, hpb)], q_snd.at[nq + i], q_rcv.at[nq + i], near)

    x_copy.wait()
    x_send.wait_recv()
    for n in range(nw):
        w_copy(n).wait()
        r = mm(x_v[...], w_v[n % WSLOT]).astype(BF16)
        for i in range(hpb):
            one = r[:nseq, i * hd:(i + 1) * hd]
            other = r[nseq:, i * hd:(i + 1) * hd]
            if n < nq:
                h = mine + hpb * n + i
                qg[h] = one
                q2[pl.ds(h, nseq, stride=PAD), :] = one.astype(F32)
                qs[hpb * n + i] = other
            else:
                kvn[n - nq, core * hpb + i] = one
                kvs[n - nq, i] = other
        if n < nq:
            q_copy(n).start()
        else:
            kv_new_copy(n - nq).start()
        if n + AHEAD < nw:
            w_copy(n + AHEAD).start()
        else:
            kv_start(n + AHEAD - nw)
    to_near.start()
    for n in range(nq):
        q_copy(n).wait_recv()
        for i in range(hpb):
            h = theirs + hpb * n + i
            q2[pl.ds(h, nseq, stride=PAD), :] = qg[h].astype(F32)

    zero8 = jnp.zeros((8, hd), F32)
    zero32 = jnp.zeros((32, hd), BF16)
    quarter = rows // 4

    def scores(slot, b, base):
        q = q2[pl.ds(pl.multiple_of(b * PAD, 8), PAD), :]
        q = jnp.concatenate([q, zero8], 0).astype(BF16)
        lhs = jnp.concatenate([jnp.concatenate([q, zero32], 1), jnp.concatenate([zero32, q], 1)], 0)
        s = []
        for p in range(2):
            k0 = k_ring[slot, base + 2 * p * quarter:base + (2 * p + 1) * quarter, :]
            k1 = k_ring[slot, base + (2 * p + 1) * quarter:base + (2 * p + 2) * quarter, :]
            r = mmt(lhs, jnp.concatenate([k0, k1], 1))
            s += [r[0:PAD], r[32:32 + PAD]]
        return s

    def weights(s, b):
        n_old = lens[b]
        s = [jnp.where(key[:, p * quarter:(p + 1) * quarter] < n_old, s[p], -jnp.inf) for p in range(4)]
        m = jnp.maximum(jnp.maximum(s[0], s[1]), jnp.maximum(s[2], s[3]))
        m = jnp.maximum(jnp.max(m, axis=1, keepdims=True), LOW)
        e = [jnp.exp2((a - m) * cs) for a in s]
        l = jnp.sum((e[0] + e[1]) + (e[2] + e[3]), axis=1, keepdims=True)
        gap = jnp.zeros((8, 2 * quarter), F32)
        w = jnp.concatenate([jnp.concatenate([e[0], e[2]], 1), gap,
                             jnp.concatenate([e[1], e[3]], 1), gap], 0).astype(BF16)
        at = pl.ds(pl.multiple_of(lax.rem(b, SUB) * PAD, 8), PAD)
        m2[at, :] = jnp.broadcast_to(m, (PAD, hd))
        l2[at, :] = jnp.broadcast_to(l, (PAD, hd))
        return w

    def values(w, slot, b, base):
        v = [v_ring[slot, base + p * quarter:base + (p + 1) * quarter, :] for p in range(4)]
        v = jnp.concatenate([jnp.concatenate([v[0], v[1]], 1), jnp.concatenate([v[2], v[3]], 1)], 0)
        o = mm(w, v)
        at = pl.ds(pl.multiple_of(lax.rem(b, SUB) * PAD, 8), PAD)
        o2[at, :] = o[0:PAD, :hd] + o[32:32 + PAD, hd:]

    def attend(g):
        slot = lax.rem(g, RING)
        s, w = {}, {}
        for n in range(GRP + 2):
            if n < GRP:
                s[n] = scores(slot, g * GRP + n, n * rows)
            if 0 <= n - 2 < GRP:
                values(w.pop(n - 2), slot, g * GRP + n - 2, (n - 2) * rows)
            if 0 <= n - 1 < GRP:
                w[n - 1] = weights(s.pop(n - 1), g * GRP + n - 1)

    def group(g, carry):
        for cp in kv_copies(g):
            cp.wait()
        attend(g)

        @pl.when(jnp.logical_and(g >= gps, g + RING < ngrp))
        def _():
            kv_start(g + RING)

        steps = [((0, 4), ()), ((4, 7), (0,)), ((7, 2 * nh), (1,)), ((), (2, 3))]
        for n, (wo_part, kv_part) in enumerate(steps):
            @pl.when(g == n)
            def _():
                for j in range(*wo_part) if wo_part else ():
                    wo_copy(j).start()
                for m in kv_part:
                    kv_start(RING + m)

        @pl.when(g == 1)
        def _():
            to_far.wait_recv()
            pass_on.start()
        return carry

    def merge(s):
        at = pl.ds(pl.multiple_of(s * SUB, SUB), SUB)

        def pre_scores(h):
            q = qg[h * grp_heads:(h + 1) * grp_heads, at, :].reshape(grp_heads * SUB, hd)
            return q, [mmt(q, kvp[n, 0, h]) for n in range(4)]

        def pre_weights(sc):
            m = jnp.maximum(jnp.maximum(sc[0], sc[1]), jnp.maximum(sc[2], sc[3]))
            m = jnp.max(m, axis=1, keepdims=True)
            e = [jnp.exp2((a - m) * cs) for a in sc]
            l = jnp.sum((e[0] + e[1]) + (e[2] + e[3]), axis=1, keepdims=True)
            return jnp.concatenate([a.astype(BF16) for a in e], 1), m, l

        def join(h, q, w, m, l):
            o = mm(w, jnp.concatenate([kvp[n, 1, h] for n in range(4)], 0))
            k_new = kvn[0, h, at, :].astype(F32)
            v_new = kvn[1, h, at, :].astype(F32)
            for i in range(grp_heads):
                part = slice(i * SUB, (i + 1) * SUB)
                rows_at = pl.ds(h * grp_heads + i, SUB, stride=PAD)
                m_s, l_s, o_s = m2[rows_at, :], l2[rows_at, :], o2[rows_at, :]
                s_n = jnp.sum(q[part].astype(F32) * k_new, axis=1, keepdims=True)
                m_p = jnp.maximum(m[part], s_n)
                m_all = jnp.maximum(m_p, m_s)
                w_p = jnp.exp2((m[part] - m_all) * cs)
                w_n = jnp.exp2((s_n - m_all) * cs)
                w_s = jnp.exp2((m_s - m_all) * cs)
                total = w_p * l[part] + w_n + w_s * l_s
                val = (w_p * o[part] + w_n * v_new + w_s * o_s) / total
                att[s, h * grp_heads + i, :SUB] = val.astype(BF16)

        sc, w = {}, {}
        for n in range(kvh + 2):
            if n < kvh:
                sc[n] = pre_scores(n)
            if 0 <= n - 2 < kvh:
                join(n - 2, *w.pop(n - 2))
            if 0 <= n - 1 < kvh:
                q, p = sc.pop(n - 1)
                w[n - 1] = (q,) + pre_weights(p)

    def att_copy(s):
        return remote(att.at[s, :, pl.ds(0, SUB)], att.at[s, :, pl.ds(SUB, SUB)], a_snd.at[s], a_rcv.at[s], near)

    def partial_copy(s, j):
        return remote(snd.at[s, j], rcv.at[s, j], f_snd.at[s, j], f_rcv.at[s, j], mate)

    def sub_rows(s):
        return pl.ds(pl.multiple_of(s * SUB, SUB), SUB)

    def y_col(j):
        return pl.ds(pl.multiple_of(t * half + core * quart + j * CB, CB), CB)

    def y_copies(s, j):
        there = out.at[sub_rows(s), y_col(j)]
        one, other = ybuf.at[s, j, pl.ds(0, SUB)], ybuf.at[s, j, pl.ds(SUB, SUB)]
        return [remote(one, there, y_snd.at[0, s, j], y_rcv.at[0, s, j], mate),
                remote(other, there, y_snd.at[1, s, j], y_rcv.at[1, s, j], diag),
                remote(other, there, y_snd.at[2, s, j], y_rcv.at[2, s, j], near)]

    def finish(s):
        def step(j, carry):
            partial_copy(s, j).wait_recv()
            y = (own[s, j] + rcv[s, j]).astype(BF16)
            ybuf[s, j] = y
            for cp in y_copies(s, j):
                cp.start()
            out[sub_rows(s), y_col(j)] = y[:SUB]
            return carry
        lax.fori_loop(0, nh, step, 0)

    def sub_pass(s, carry):
        lax.fori_loop(s * gps, (s + 1) * gps, group, 0)

        @pl.when(s == 0)
        def _():
            to_near.wait_recv()
            for i in range(2):
                kv_new_copy(i).wait_recv()
            pass_on.wait_recv()

        merge(s)
        att_copy(s).start()

        @pl.when(s > 0)
        def _():
            finish(s - 1)
        att_copy(s).wait_recv()

        def wo_wait(j):
            @pl.when(s == 0)
            def _():
                wo_copy(2 * j).wait()
                wo_copy(2 * j + 1).wait()

        def keep(j, p):
            x_at = jnp.concatenate([x_v[sub_rows(s), y_col(j)],
                                    x_v[pl.ds(pl.multiple_of(nseq + s * SUB, SUB), SUB), y_col(j)]], 0)
            own[s, j] = p + x_at.astype(F32)

        a = jnp.concatenate([att[s, h] for h in range(heads)], 1)
        for j in range(nh):
            wo_wait(j)
            p = mm(a, wo_v[j])
            for i in range(2):
                n = 2 * j + i
                if n < nh:
                    snd[s, n] = p[:, i * CB:(i + 1) * CB]
                    partial_copy(s, n).start()
                else:
                    keep(n - nh, p[:, i * CB:(i + 1) * CB])
        return carry

    lax.fori_loop(0, nsub, sub_pass, 0)
    finish(nsub - 1)

    def drain(n, carry):
        s, j = n // nh, lax.rem(n, nh)
        partial_copy(s, j).wait_send()
        for cp in y_copies(s, j):
            cp.wait()
        return carry
    lax.fori_loop(0, nsub * nh, drain, 0)
    for s in range(nsub):
        att_copy(s).wait_send()
    for n in range(nq):
        q_copy(n).wait_send()
    for i in range(2):
        kv_new_copy(i).wait_send()
    x_send.wait_send()
    to_far.wait_send()
    to_near.wait_send()
    pass_on.wait_send()


def solution(mesh):
    row_axes = ('dp', 'ctx')

    def device_step(hidden, w_q, w_k, w_v, w_o, k_prefix, v_prefix, k_suffix, v_suffix, seq_lens):
        nseq, model = hidden.shape
        npos, kvh, hd = k_prefix.shape
        slots = k_suffix.shape[1]
        heads = w_q.shape[1] // hd
        rows = slots * kvh
        nsub, nh = nseq // SUB, model // 4 // CB
        nw = heads * hd // 2 // CB + 2
        hpb = CB // hd
        dims = (nseq, model, heads, kvh, hd, slots)
        hbm = pl.BlockSpec(memory_space=pl.ANY)
        dma = pltpu.SemaphoreType.DMA
        return pl.pallas_call(
            functools.partial(body, dims),
            out_shape=jax.ShapeDtypeStruct((nseq, model), BF16),
            in_specs=[hbm] * 9 + [pl.BlockSpec(memory_space=pltpu.SMEM)],
            out_specs=pl.BlockSpec(memory_space=pltpu.VMEM),
            scratch_shapes=[
                pltpu.VMEM((2 * nseq, model), BF16),
                pltpu.VMEM((WSLOT, model, CB), BF16),
                pltpu.VMEM((nh, heads * hd, 2 * CB), BF16),
                pltpu.VMEM((RING, GRP * rows, hd), BF16),
                pltpu.VMEM((RING, GRP * rows, hd), BF16),
                pltpu.VMEM((nseq * PAD, hd), F32),
                pltpu.VMEM((heads, nseq, hd), BF16),
                pltpu.VMEM((heads // 2, nseq, hd), BF16),
                pltpu.VMEM((2, kvh, nseq, hd), BF16),
                pltpu.VMEM((2, hpb, nseq, hd), BF16),
                pltpu.VMEM((npos * kvh, hd), F32),
                pltpu.VMEM((4, 2, kvh, npos, hd), BF16),
                pltpu.VMEM((PAD, rows), jnp.int32),
                pltpu.VMEM((SUB * PAD, hd), F32),
                pltpu.VMEM((SUB * PAD, hd), F32),
                pltpu.VMEM((SUB * PAD, hd), F32),
                pltpu.VMEM((nsub, heads, 2 * SUB, hd), BF16),
                pltpu.VMEM((nsub, nh, 2 * SUB, CB), F32),
                pltpu.VMEM((nsub, nh, 2 * SUB, CB), F32),
                pltpu.VMEM((nsub, nh, 2 * SUB, CB), F32),
                pltpu.VMEM((nsub, nh, 2 * SUB, CB), BF16),
                dma((3,)), dma((2,)), dma((nw,)), dma((2 * nh,)), dma((RING, 2)),
                dma((3,)), dma((3,)), dma((nw,)), dma((nw,)), dma((nsub,)), dma((nsub,)),
                dma((nsub, nh)), dma((nsub, nh)), dma((3, nsub, nh)), dma((3, nsub, nh)),
            ],
            compiler_params=pltpu.CompilerParams(collective_id=0, has_side_effects=True,
                                                 vmem_limit_bytes=67043328),
        )(hidden, w_q, w_k, w_v, w_o,
          k_prefix.reshape(npos * kvh, hd), v_prefix.reshape(npos * kvh, hd),
          k_suffix.reshape(nseq * rows, hd), v_suffix.reshape(nseq * rows, hd), seq_lens)

    spec_in = (P(row_axes, None), P(None, 'tp'), P(None, 'tp'), P(None, 'tp'), P('tp', None), P(row_axes, 'tp', None), P(row_axes, 'tp', None), P(row_axes, None, 'tp', None), P(row_axes, None, 'tp', None), P(row_axes))
    return jax.shard_map(device_step, mesh=mesh, in_specs=spec_in, out_specs=P(row_axes, None), check_vma=False)
```

time: 85.4 us -> 78.1 us (0.915)
  Pallas kernels: 82.8 us -> 75.5 us
    pallas_call x1, Pallas kernels: 82.8 us -> 75.5 us  [device_step(): pl.pallas_call(functools.partial(body, dims), out_shape=jax.ShapeDtypeStr...]
where the time goes in v3:
time: 78.1 us; the launch traced here: 78 us
  Pallas kernels  75.5 us (97%)
  local copies, waits for them, and re-layouts  2.46 us (3%)
    pallas_call x1, Pallas kernels, device_step(): pl.pallas_call(functools.partial(body, dims), out_shape=jax.ShapeDtypeStr...  75.5 us
    unnamed x1, local copies, waits for them, and re-layouts  2.46 us

profile of v3, /device:TPU:0, one launch (start us, length us, event | category | flops | bytes accessed | tf_op | source)
XLA Modules:
  0.0 78.0 jit_solution(2246089333685134645)
XLA Ops:
  0.0 75.5 %shard_map.100 = bf16[128,5120]{1,0:T(8,128)(2,1)} custom-call(bf16[128,5120]{1,0:T(8,128)(2,1)} %hid.1, bf16[5120,2560]{1,0:T(8,128)(2,1)} %wq.1, bf16[5120,512]{1,0:T(8,128)(2,1)} %wk.1, bf16[5120,512]{1,0:T(8,128)(2,1)} %wv.1, bf16[2560,5120]{1,0:T(8,128)(2,1)} %wo.1, bf16[1024,128]{1,0:T(8,128)(2,1)} %bitcast.6, bf16[1024,128]{1,0:T(8,128)(2,1)} %bitcast.7, ...), custom_call_target="tpu_custom_call" | custom-call | tf_op jit(solution)/shard_map/pallas_call | solution.py:385
  75.5 2.5 %copy.12 = bf16[128,5120]{1,0:T(8,128)(2,1)} copy(bf16[128,5120]{1,0:T(8,128)(2,1)} %shard_map.100) | data formatting | bytes 2621440

commit v4 on v3

v4 whole, which is shorter than its diff:
```python
import functools

import jax
import jax.numpy as jnp
from jax import lax
from jax.experimental import pallas as pl
from jax.experimental.pallas import tpu as pltpu
from jax.sharding import PartitionSpec as P

MESH = pl.DeviceIdType.MESH
F32 = jnp.float32
BF16 = jnp.bfloat16
LOG2E = 1.4426950408889634
LOW = -3.0e38

CB = 256
PASSES = (32, 32, 32, 32)
GRP = 8
RING = 4
AHEAD = 4
PAD = 24


def mm(a, b):
    return jnp.dot(a, b, preferred_element_type=F32)


def mmt(a, b):
    return lax.dot_general(a, b, (((1,), (1,)), ((), ())), preferred_element_type=F32)


def body(dims, hid, wq, wk, wv, wo, kp, vp, ks, vs, lens, out,
         x_v, w_v, wo_v, k_ring, v_ring, q2, qg, qs, kvn, kvs, kvp, key,
         o2, m2, att, snd, rcv, own, ybuf,
         x_sem, p_sem, n_sem, w_sem, wo_sem, kv_sem, g_snd, g_rcv, q_snd, q_rcv, a_snd, a_rcv,
         f_snd, f_rcv, y_snd, y_rcv):
    nseq, model, heads, kvh, hd, slots = dims
    grp_heads = heads // kvh
    rows = slots * kvh
    half = model // 2
    quart = half // 2
    nq = heads * hd // 2 // CB
    nw = nq + 2
    nh = quart // CB
    ngrp = nseq // GRP
    starts = [sum(PASSES[:p]) for p in range(len(PASSES))]
    npos = kvp.shape[3]
    c = lax.axis_index('ctx')
    t = lax.axis_index('tp')
    core = lax.rem(c, 2)
    sib = c + 1 - 2 * core
    far = {'ctx': lax.rem(c + 2, 4)}
    near = {'ctx': sib}
    mate = {'tp': 1 - t}
    diag = {'tp': 1 - t, 'ctx': sib}
    cs = LOG2E * hd ** -0.5

    def remote(src, dst, ss, rs, dev):
        return pltpu.make_async_remote_copy(src_ref=src, dst_ref=dst, send_sem=ss, recv_sem=rs,
                                            device_id=dev, device_id_type=MESH)

    def w_copy(n):
        if n < nq:
            src, col = wq, core * (nq * CB) + n * CB
        else:
            src, col = (wk, wv)[n - nq], core * CB
        return pltpu.make_async_copy(src.at[:, pl.ds(pl.multiple_of(col, CB), CB)], w_v.at[n], w_sem.at[n])

    def wo_copy(j):
        side = (1 - t) if j < nh else t
        col = side * half + core * quart + (j % nh) * CB
        return pltpu.make_async_copy(wo.at[:, pl.ds(pl.multiple_of(col, CB), CB)],
                                     wo_v.at[j // 2, :, pl.ds(j % 2 * CB, CB)], wo_sem.at[j])

    def kv_copies(g):
        slot = lax.rem(g, RING)
        src = pl.ds(g * GRP * rows, GRP * rows)
        return [pltpu.make_async_copy(ks.at[src], k_ring.at[slot], kv_sem.at[slot, 0]),
                pltpu.make_async_copy(vs.at[src], v_ring.at[slot], kv_sem.at[slot, 1])]

    def kv_start(g):
        for cp in kv_copies(g):
            cp.start()

    pre = [k_ring.at[RING - 1, pl.ds(0, npos * kvh)], v_ring.at[RING - 1, pl.ds(0, npos * kvh)]]
    x_copy = pltpu.make_async_copy(hid, x_v.at[pl.ds(0, nseq)], x_sem.at[0])
    p_copies = [pltpu.make_async_copy(kp, pre[0], p_sem.at[0]), pltpu.make_async_copy(vp, pre[1], p_sem.at[1])]

    barrier = pltpu.get_barrier_semaphore()
    for dev in (near, far, mate, diag):
        pl.semaphore_signal(barrier, inc=1, device_id=dev, device_id_type=MESH)
    p_copies[0].start()
    p_copies[1].start()
    x_copy.start()
    for n in range(AHEAD):
        w_copy(n).start()

    dei = q2.at[pl.ds(0, npos * kvh)]
    for i in range(2):
        p_copies[i].wait()
        dei[...] = pre[i][...].astype(F32)
        for h in range(kvh):
            kvp[0, h, i] = dei[pl.ds(h, npos, stride=kvh), :].astype(BF16)
    to_far = [remote(kvp.at[0, h], kvp.at[2, h], g_snd.at[0, h], g_rcv.at[0, h], far) for h in range(kvh)]
    pass_on = [remote(kvp.at[2, h], kvp.at[3, h], g_snd.at[1, h], g_rcv.at[1, h], near) for h in range(kvh)]
    to_near = remote(kvp.at[0], kvp.at[1], n_sem.at[0], n_sem.at[1], near)
    x_send = remote(x_v.at[pl.ds(0, nseq)], x_v.at[pl.ds(nseq, nseq)], x_sem.at[1], x_sem.at[2], near)
    x_copy.wait()
    pl.semaphore_wait(barrier, 4)
    for cp in to_far:
        cp.start()
    x_send.start()

    row_head = lax.broadcasted_iota(jnp.int32, (PAD, rows), 0) // grp_heads
    col_row = lax.broadcasted_iota(jnp.int32, (PAD, rows), 1)
    key[...] = jnp.where(lax.rem(col_row, kvh) == row_head, col_row // kvh, slots)
    for h in range(heads, PAD):
        q2[pl.ds(h, nseq, stride=PAD), :] = jnp.zeros((nseq, hd), F32)

    hpb = CB // hd
    mine = core * (nq * hpb)
    theirs = (1 - core) * (nq * hpb)

    def q_copy(n):
        at = pl.ds(hpb * n, hpb)
        return remote(qs.at[at], qg.at[pl.ds(mine + hpb * n, hpb)], q_snd.at[n], q_rcv.at[n], near)

    def kv_new_copy(i):
        return remote(kvs.at[i], kvn.at[i, pl.ds(core * hpb, hpb)], q_snd.at[nq + i], q_rcv.at[nq + i], near)

    def rows_dot(lo, n):
        r = [mm(x_v[lo + i * (nseq // 2):lo + (i + 1) * (nseq // 2)], w_v[n]) for i in range(2)]
        return jnp.concatenate(r, 0).astype(BF16)

    for n in range(nw):
        w_copy(n).wait()
        r = rows_dot(0, n)
        for i in range(hpb):
            one = r[:, i * hd:(i + 1) * hd]
            if n < nq:
                h = mine + hpb * n + i
                qg[h] = one
                q2[pl.ds(h, nseq, stride=PAD), :] = one.astype(F32)
            else:
                kvn[n - nq, core * hpb + i] = one
        if n + AHEAD < nw:
            w_copy(n + AHEAD).start()
        else:
            kv_start(n + AHEAD - nw)
    x_send.wait_recv()
    for n in range(nw):
        r = rows_dot(nseq, n)
        for i in range(hpb):
            one = r[:, i * hd:(i + 1) * hd]
            if n < nq:
                qs[hpb * n + i] = one
            else:
                kvs[n - nq, i] = one
        if n < nq:
            q_copy(n).start()
        else:
            kv_new_copy(n - nq).start()
    to_near.start()
    for n in range(nq):
        q_copy(n).wait_recv()
        for i in range(hpb):
            h = theirs + hpb * n + i
            q2[pl.ds(h, nseq, stride=PAD), :] = qg[h].astype(F32)

    zero8 = jnp.zeros((8, hd), F32)
    zero32 = jnp.zeros((32, hd), BF16)
    quarter = rows // 4

    def scores(slot, b, base):
        q = q2[pl.ds(pl.multiple_of(b * PAD, 8), PAD), :]
        q = jnp.concatenate([q, zero8], 0).astype(BF16)
        lhs = jnp.concatenate([jnp.concatenate([q, zero32], 1), jnp.concatenate([zero32, q], 1)], 0)
        s = []
        for p in range(2):
            k0 = k_ring[slot, base + 2 * p * quarter:base + (2 * p + 1) * quarter, :]
            k1 = k_ring[slot, base + (2 * p + 1) * quarter:base + (2 * p + 2) * quarter, :]
            r = mmt(lhs, jnp.concatenate([k0, k1], 1))
            s += [r[0:PAD], r[32:32 + PAD]]
        return s

    def weights(s, b):
        n_old = lens[b]
        s = [jnp.where(key[:, p * quarter:(p + 1) * quarter] < n_old, s[p], -jnp.inf) for p in range(4)]
        m = jnp.maximum(jnp.maximum(s[0], s[1]), jnp.maximum(s[2], s[3]))
        m = jnp.maximum(jnp.max(m, axis=1, keepdims=True), LOW)
        e = [jnp.exp2((a - m) * cs) for a in s]
        l = jnp.sum((e[0] + e[1]) + (e[2] + e[3]), axis=1, keepdims=True)
        gap = jnp.zeros((8, 2 * quarter), F32)
        w = jnp.concatenate([jnp.concatenate([e[0], e[2]], 1), gap,
                             jnp.concatenate([e[1], e[3]], 1), gap], 0).astype(BF16)
        return w, m, l

    def values(w, m, l, slot, base, local):
        v = [v_ring[slot, base + p * quarter:base + (p + 1) * quarter, :] for p in range(4)]
        v = jnp.concatenate([jnp.concatenate([v[0], v[1]], 1), jnp.concatenate([v[2], v[3]], 1)], 0)
        o = mm(w, v)
        at = pl.ds(pl.multiple_of(local * PAD, 8), PAD)
        o2[at, :] = (o[0:PAD, :hd] + o[32:32 + PAD, hd:]) / jnp.maximum(l, 1.0)
        m2[at, :] = jnp.broadcast_to(m + jnp.log2(l) / cs, (PAD, hd))

    per = 2 * GRP

    def attend(d, first):
        for i in range(2):
            for cp in kv_copies(2 * d + i):
                cp.wait()
        slots_of = [lax.rem(2 * d + i, RING) for i in range(2)]
        s, w = {}, {}
        for n in range(per + 2):
            if n < per:
                s[n] = scores(slots_of[n // GRP], d * per + n, n % GRP * rows)
            if 0 <= n - 2 < per:
                m = n - 2
                values(*w.pop(m), slots_of[m // GRP], m % GRP * rows, d * per + m - first)
            if 0 <= n - 1 < per:
                w[n - 1] = weights(s.pop(n - 1), d * per + n - 1)

    def refill(d):
        for i in range(2):
            kv_start(2 * d + RING + i)

    def merge(p, before):
        size, lo = PASSES[p], starts[p]
        at = pl.ds(lo, size)

        def pre_scores(h):
            q = qg[h * grp_heads:(h + 1) * grp_heads, at, :].reshape(grp_heads * size, hd)
            return q, [mmt(q, kvp[n, h, 0]) for n in range(4)]

        def pre_weights(sc):
            m = jnp.maximum(jnp.maximum(sc[0], sc[1]), jnp.maximum(sc[2], sc[3]))
            m = jnp.max(m, axis=1, keepdims=True)
            e = [jnp.exp2((a - m) * cs) for a in sc]
            l = jnp.sum((e[0] + e[1]) + (e[2] + e[3]), axis=1, keepdims=True)
            return jnp.concatenate([a.astype(BF16) for a in e], 1), m, l

        def join(h, q, w, m, l):
            o = mm(w, jnp.concatenate([kvp[n, h, 1] for n in range(4)], 0))
            k_new = kvn[0, h, at, :].astype(F32)
            v_new = kvn[1, h, at, :].astype(F32)
            for i in range(grp_heads):
                part = slice(i * size, (i + 1) * size)
                rows_at = pl.ds(h * grp_heads + i, size, stride=PAD)
                m_s, o_s = m2[rows_at, :], o2[rows_at, :]
                s_n = jnp.sum(q[part].astype(F32) * k_new, axis=1, keepdims=True)
                m_p = jnp.maximum(m[part], s_n)
                m_all = jnp.maximum(m_p, m_s)
                w_p = jnp.exp2((m[part] - m_all) * cs)
                w_n = jnp.exp2((s_n - m_all) * cs)
                w_s = jnp.exp2((m_s - m_all) * cs)
                total = w_p * l[part] + w_n + w_s
                val = (w_p * o[part] + w_n * v_new + w_s * o_s) / total
                att[h * grp_heads + i, 2 * lo:2 * lo + size] = val.astype(BF16)

        sc, w = {}, {}
        for n in range(kvh + 2):
            if n < kvh:
                before(n)
                sc[n] = pre_scores(n)
            if 0 <= n - 2 < kvh:
                join(n - 2, *w.pop(n - 2))
                att_copy(p, n - 2).start()
            if 0 <= n - 1 < kvh:
                q, part = sc.pop(n - 1)
                w[n - 1] = (q,) + pre_weights(part)

    def att_copy(p, h):
        heads_at = pl.ds(h * grp_heads, grp_heads)
        lo, size = 2 * starts[p], PASSES[p]
        return remote(att.at[heads_at, pl.ds(lo, size)], att.at[heads_at, pl.ds(lo + size, size)],
                      a_snd.at[p, h], a_rcv.at[p, h], near)

    def both(p):
        return pl.ds(2 * starts[p], 2 * PASSES[p])

    def partial_copy(p, j):
        return remote(snd.at[j, both(p)], rcv.at[j, both(p)], f_snd.at[p, j], f_rcv.at[p, j], mate)

    def y_col(j):
        return pl.ds(pl.multiple_of(t * half + core * quart + j * CB, CB), CB)

    def y_copies(p, j):
        size = PASSES[p]
        there = out.at[pl.ds(starts[p], size), y_col(j)]
        one, other = [ybuf.at[j, pl.ds(2 * starts[p] + i * size, size)] for i in range(2)]
        return [remote(one, there, y_snd.at[0, p, j], y_rcv.at[0, p, j], mate),
                remote(other, there, y_snd.at[1, p, j], y_rcv.at[1, p, j], diag),
                remote(other, there, y_snd.at[2, p, j], y_rcv.at[2, p, j], near)]

    def finish(p):
        for j in range(nh):
            partial_copy(p, j).wait_recv()
            y = (own[j, both(p)] + rcv[j, both(p)]).astype(BF16)
            ybuf[j, both(p)] = y
            for cp in y_copies(p, j):
                cp.start()
            out[pl.ds(starts[p], PASSES[p]), y_col(j)] = y[:PASSES[p]]

    def project(p):
        size, lo = PASSES[p], starts[p]
        for h in range(kvh):
            att_copy(p, h).wait_recv()
        a = jnp.concatenate([att[h, both(p)] for h in range(heads)], 1)
        for j in range(nh):
            if p == 0:
                wo_copy(2 * j).wait()
                wo_copy(2 * j + 1).wait()
            r = mm(a, wo_v[j])
            for i in range(2):
                n = 2 * j + i
                part = r[:, i * CB:(i + 1) * CB]
                if n < nh:
                    snd[n, both(p)] = part
                    partial_copy(p, n).start()
                else:
                    x_at = jnp.concatenate([x_v[pl.ds(lo, size), y_col(n - nh)],
                                            x_v[pl.ds(nseq + lo, size), y_col(n - nh)]], 0)
                    own[n - nh, both(p)] = part + x_at.astype(F32)

    def forward(h):
        to_far[h].wait_recv()
        pass_on[h].start()

    def need(h):
        if h == 0:
            to_near.wait_recv()
            for i in range(2):
                kv_new_copy(i).wait_recv()
        if h == 2:
            forward(kvh - 1)
        pass_on[h].wait_recv()

    npass = len(PASSES)
    for p in range(npass):
        d0, d1 = starts[p] // per, (starts[p] + PASSES[p]) // per
        if p == 0:
            forward(0)
            for d in range(d0, d1):
                attend(d, 0)
                refill(d)
                if d < 2:
                    for j in range(nh * d, nh * (d + 1)):
                        wo_copy(j).start()
                    forward(1 + d)
            merge(p, need)
        else:
            def step(d, carry):
                attend(d, starts[p])

                @pl.when(2 * d + RING < ngrp)
                def _():
                    refill(d)
                return carry
            lax.fori_loop(d0, d1, step, 0)
            merge(p, lambda h: None)
        project(p)
        if p > 0:
            finish(p - 1)
    finish(npass - 1)

    for p in range(npass):
        for j in range(nh):
            partial_copy(p, j).wait_send()
            for cp in y_copies(p, j):
                cp.wait()
        for h in range(kvh):
            att_copy(p, h).wait_send()
    for n in range(nq):
        q_copy(n).wait_send()
    for i in range(2):
        kv_new_copy(i).wait_send()
    x_send.wait_send()
    to_near.wait_send()
    for h in range(kvh):
        to_far[h].wait_send()
        pass_on[h].wait_send()


def solution(mesh):
    row_axes = ('dp', 'ctx')

    def device_step(hidden, w_q, w_k, w_v, w_o, k_prefix, v_prefix, k_suffix, v_suffix, seq_lens):
        nseq, model = hidden.shape
        npos, kvh, hd = k_prefix.shape
        slots = k_suffix.shape[1]
        heads = w_q.shape[1] // hd
        rows = slots * kvh
        npass, nh = len(PASSES), model // 4 // CB
        nw = heads * hd // 2 // CB + 2
        hpb = CB // hd
        dims = (nseq, model, heads, kvh, hd, slots)
        hbm = pl.BlockSpec(memory_space=pl.ANY)
        dma = pltpu.SemaphoreType.DMA
        return pl.pallas_call(
            functools.partial(body, dims),
            out_shape=jax.ShapeDtypeStruct((nseq, model), BF16),
            in_specs=[hbm] * 9 + [pl.BlockSpec(memory_space=pltpu.SMEM)],
            out_specs=pl.BlockSpec(memory_space=pltpu.VMEM),
            scratch_shapes=[
                pltpu.VMEM((2 * nseq, model), BF16),
                pltpu.VMEM((nw, model, CB), BF16),
                pltpu.VMEM((nh, heads * hd, 2 * CB), BF16),
                pltpu.VMEM((RING, GRP * rows, hd), BF16),
                pltpu.VMEM((RING, GRP * rows, hd), BF16),
                pltpu.VMEM((nseq * PAD, hd), F32),
                pltpu.VMEM((heads, nseq, hd), BF16),
                pltpu.VMEM((heads // 2, nseq, hd), BF16),
                pltpu.VMEM((2, kvh, nseq, hd), BF16),
                pltpu.VMEM((2, hpb, nseq, hd), BF16),
                pltpu.VMEM((4, kvh, 2, npos, hd), BF16),
                pltpu.VMEM((PAD, rows), jnp.int32),
                pltpu.VMEM((max(PASSES) * PAD, hd), F32),
                pltpu.VMEM((max(PASSES) * PAD, hd), F32),
                pltpu.VMEM((heads, 2 * nseq, hd), BF16),
                pltpu.VMEM((nh, 2 * nseq, CB), F32),
                pltpu.VMEM((nh, 2 * nseq, CB), F32),
                pltpu.VMEM((nh, 2 * nseq, CB), F32),
                pltpu.VMEM((nh, 2 * nseq, CB), BF16),
                dma((3,)), dma((2,)), dma((2,)), dma((nw,)), dma((2 * nh,)), dma((RING, 2)),
                dma((2, kvh)), dma((2, kvh)), dma((nw,)), dma((nw,)), dma((npass, kvh)), dma((npass, kvh)),
                dma((npass, nh)), dma((npass, nh)), dma((3, npass, nh)), dma((3, npass, nh)),
            ],
            compiler_params=pltpu.CompilerParams(collective_id=0, has_side_effects=True,
                                                 vmem_limit_bytes=67043328),
        )(hidden, w_q, w_k, w_v, w_o,
          k_prefix.reshape(npos * kvh, hd), v_prefix.reshape(npos * kvh, hd),
          k_suffix.reshape(nseq * rows, hd), v_suffix.reshape(nseq * rows, hd), seq_lens)

    spec_in = (P(row_axes, None), P(None, 'tp'), P(None, 'tp'), P(None, 'tp'), P('tp', None), P(row_axes, 'tp', None), P(row_axes, 'tp', None), P(row_axes, None, 'tp', None), P(row_axes, None, 'tp', None), P(row_axes))
    return jax.shard_map(device_step, mesh=mesh, in_specs=spec_in, out_specs=P(row_axes, None), check_vma=False)
```

time: 78.1 us -> 84.7 us (1.085)
  Pallas kernels: 75.5 us -> 82.1 us
    pallas_call x1, Pallas kernels: 75.5 us -> 82.1 us  [device_step(): pl.pallas_call(functools.partial(body, dims), out_shape=jax.ShapeDtypeStr...]
where the time goes in v4:
time: 84.7 us; the launch traced here: 84.5 us
  Pallas kernels  82.1 us (97%)
  local copies, waits for them, and re-layouts  2.46 us (3%)
    pallas_call x1, Pallas kernels, device_step(): pl.pallas_call(functools.partial(body, dims), out_shape=jax.ShapeDtypeStr...  82.1 us
    unnamed x1, local copies, waits for them, and re-layouts  2.46 us

profile of v4, /device:TPU:0, one launch (start us, length us, event | category | flops | bytes accessed | tf_op | source)
XLA Modules:
  0.0 84.5 jit_solution(1724965750126455079)
XLA Ops:
  0.0 82.1 %shard_map.100 = bf16[128,5120]{1,0:T(8,128)(2,1)} custom-call(bf16[128,5120]{1,0:T(8,128)(2,1)} %hid.1, bf16[5120,2560]{1,0:T(8,128)(2,1)} %wq.1, bf16[5120,512]{1,0:T(8,128)(2,1)} %wk.1, bf16[5120,512]{1,0:T(8,128)(2,1)} %wv.1, bf16[2560,5120]{1,0:T(8,128)(2,1)} %wo.1, bf16[1024,128]{1,0:T(8,128)(2,1)} %bitcast.6, bf16[1024,128]{1,0:T(8,128)(2,1)} %bitcast.7, ...), custom_call_target="tpu_custom_call" | custom-call | tf_op jit(solution)/shard_map/pallas_call | solution.py:399
  82.1 2.5 %copy.12 = bf16[128,5120]{1,0:T(8,128)(2,1)} copy(bf16[128,5120]{1,0:T(8,128)(2,1)} %shard_map.100) | data formatting | bytes 2621440

commit v5 on v4

--- a/solution.py
+++ b/solution.py
@@ -14,10 +14,10 @@
 LOW = -3.0e38
 
 CB = 256
-PASSES = (32, 32, 32, 32)
+SUB = 32
 GRP = 8
 RING = 4
-AHEAD = 4
+AHEAD = 3
 PAD = 24
 
 
@@ -31,7 +31,7 @@
 
 def body(dims, hid, wq, wk, wv, wo, kp, vp, ks, vs, lens, out,
          x_v, w_v, wo_v, k_ring, v_ring, q2, qg, qs, kvn, kvs, kvp, key,
-         o2, m2, att, snd, rcv, own, ybuf,
+         o2, m2, snd, rcv, own,
          x_sem, p_sem, n_sem, w_sem, wo_sem, kv_sem, g_snd, g_rcv, q_snd, q_rcv, a_snd, a_rcv,
          f_snd, f_rcv, y_snd, y_rcv):
     nseq, model, heads, kvh, hd, slots = dims
@@ -43,7 +43,7 @@
     nw = nq + 2
     nh = quart // CB
     ngrp = nseq // GRP
-    starts = [sum(PASSES[:p]) for p in range(len(PASSES))]
+    npass = nseq // SUB
     npos = kvp.shape[3]
     c = lax.axis_index('ctx')
     t = lax.axis_index('tp')
@@ -128,13 +128,10 @@
     def kv_new_copy(i):
         return remote(kvs.at[i], kvn.at[i, pl.ds(core * hpb, hpb)], q_snd.at[nq + i], q_rcv.at[nq + i], near)
 
-    def rows_dot(lo, n):
-        r = [mm(x_v[lo + i * (nseq // 2):lo + (i + 1) * (nseq // 2)], w_v[n]) for i in range(2)]
-        return jnp.concatenate(r, 0).astype(BF16)
-
-    for n in range(nw):
-        w_copy(n).wait()
-        r = rows_dot(0, n)
+    def block_dot(lo, n):
+        return mm(x_v[lo:lo + nseq], w_v[n]).astype(BF16)
+
+    def put_own(n, r):
         for i in range(hpb):
             one = r[:, i * hd:(i + 1) * hd]
             if n < nq:
@@ -143,13 +140,8 @@
                 q2[pl.ds(h, nseq, stride=PAD), :] = one.astype(F32)
             else:
                 kvn[n - nq, core * hpb + i] = one
-        if n + AHEAD < nw:
-            w_copy(n + AHEAD).start()
-        else:
-            kv_start(n + AHEAD - nw)
-    x_send.wait_recv()
-    for n in range(nw):
-        r = rows_dot(nseq, n)
+
+    def put_other(n, r):
         for i in range(hpb):
             one = r[:, i * hd:(i + 1) * hd]
             if n < nq:
@@ -160,6 +152,23 @@
             q_copy(n).start()
         else:
             kv_new_copy(n - nq).start()
+
+    todo = [(0, n) for n in range(nw)] + [(nseq, n) for n in range(nw)]
+    for i in range(0, len(todo), 2):
+        pair = todo[i:i + 2]
+        for lo, n in pair:
+            if lo == 0:
+                w_copy(n).wait()
+                if n + AHEAD < nw:
+                    w_copy(n + AHEAD).start()
+                else:
+                    kv_start(n + AHEAD - nw)
+            elif n == 0:
+                x_send.wait_recv()
+        r = [block_dot(lo, n) for lo, n in pair]
+        for (lo, n), one in zip(pair, r):
+            (put_other if lo else put_own)(n, one)
+    kv_start(RING - 1)
     to_near.start()
     for n in range(nq):
         q_copy(n).wait_recv()
@@ -224,9 +233,27 @@
         for i in range(2):
             kv_start(2 * d + RING + i)
 
-    def merge(p, before):
-        size, lo = PASSES[p], starts[p]
-        at = pl.ds(lo, size)
+    ybuf = w_v.at[0]
+
+    def at_rows(lo, step, size):
+        return pl.ds(lo if isinstance(lo, int) else pl.multiple_of(lo, step), size)
+
+    def att_at(p, side, h, count):
+        lo = 2 * p * SUB * heads + (side * heads + h) * SUB
+        return w_v.at[1, at_rows(lo, SUB, count * SUB), pl.ds(0, hd)]
+
+    def seqs(p):
+        return at_rows(p * SUB, SUB, SUB)
+
+    def both(p):
+        return at_rows(2 * p * SUB, 2 * SUB, 2 * SUB)
+
+    def y_rows(p, j, side, count):
+        return at_rows(2 * (j * nseq + p * SUB) + side * SUB, SUB, count * SUB)
+
+    def merge(p, some, before=lambda h: None):
+        size = SUB
+        at = seqs(p)
 
         def pre_scores(h):
             q = qg[h * grp_heads:(h + 1) * grp_heads, at, :].reshape(grp_heads * size, hd)
@@ -255,28 +282,23 @@
                 w_s = jnp.exp2((m_s - m_all) * cs)
                 total = w_p * l[part] + w_n + w_s
                 val = (w_p * o[part] + w_n * v_new + w_s * o_s) / total
-                att[h * grp_heads + i, 2 * lo:2 * lo + size] = val.astype(BF16)
+                att_at(p, 0, h * grp_heads + i, 1)[...] = val.astype(BF16)
 
         sc, w = {}, {}
-        for n in range(kvh + 2):
-            if n < kvh:
-                before(n)
-                sc[n] = pre_scores(n)
-            if 0 <= n - 2 < kvh:
-                join(n - 2, *w.pop(n - 2))
-                att_copy(p, n - 2).start()
-            if 0 <= n - 1 < kvh:
+        for n in range(len(some) + 2):
+            if n < len(some):
+                before(some[n])
+                sc[n] = pre_scores(some[n])
+            if 0 <= n - 2:
+                join(some[n - 2], *w.pop(n - 2))
+                att_copy(p, some[n - 2]).start()
+            if 0 <= n - 1 < len(some):
                 q, part = sc.pop(n - 1)
                 w[n - 1] = (q,) + pre_weights(part)
 
     def att_copy(p, h):
-        heads_at = pl.ds(h * grp_heads, grp_heads)
-        lo, size = 2 * starts[p], PASSES[p]
-        return remote(att.at[heads_at, pl.ds(lo, size)], att.at[heads_at, pl.ds(lo + size, size)],
-                      a_snd.at[p, h], a_rcv.at[p, h], near)
-
-    def both(p):
-        return pl.ds(2 * starts[p], 2 * PASSES[p])
+        mine_at, theirs_at = [att_at(p, side, h * grp_heads, grp_heads) for side in range(2)]
+        return remote(mine_at, theirs_at, a_snd.at[p, h], a_rcv.at[p, h], near)
 
     def partial_copy(p, j):
         return remote(snd.at[j, both(p)], rcv.at[j, both(p)], f_snd.at[p, j], f_rcv.at[p, j], mate)
@@ -285,9 +307,8 @@
         return pl.ds(pl.multiple_of(t * half + core * quart + j * CB, CB), CB)
 
     def y_copies(p, j):
-        size = PASSES[p]
-        there = out.at[pl.ds(starts[p], size), y_col(j)]
-        one, other = [ybuf.at[j, pl.ds(2 * starts[p] + i * size, size)] for i in range(2)]
+        there = out.at[seqs(p), y_col(j)]
+        one, other = [ybuf.at[y_rows(p, j, side, 1)] for side in range(2)]
         return [remote(one, there, y_snd.at[0, p, j], y_rcv.at[0, p, j], mate),
                 remote(other, there, y_snd.at[1, p, j], y_rcv.at[1, p, j], diag),
                 remote(other, there, y_snd.at[2, p, j], y_rcv.at[2, p, j], near)]
@@ -296,18 +317,18 @@
         for j in range(nh):
             partial_copy(p, j).wait_recv()
             y = (own[j, both(p)] + rcv[j, both(p)]).astype(BF16)
-            ybuf[j, both(p)] = y
+            ybuf[y_rows(p, j, 0, 2)] = y
             for cp in y_copies(p, j):
                 cp.start()
-            out[pl.ds(starts[p], PASSES[p]), y_col(j)] = y[:PASSES[p]]
-
-    def project(p):
-        size, lo = PASSES[p], starts[p]
+            out[seqs(p), y_col(j)] = y[:SUB]
+
+    def project(p, first):
         for h in range(kvh):
             att_copy(p, h).wait_recv()
-        a = jnp.concatenate([att[h, both(p)] for h in range(heads)], 1)
+        a = jnp.concatenate([jnp.concatenate([att_at(p, side, h, 1)[...] for side in range(2)], 0)
+                             for h in range(heads)], 1)
         for j in range(nh):
-            if p == 0:
+            if first:
                 wo_copy(2 * j).wait()
                 wo_copy(2 * j + 1).wait()
             r = mm(a, wo_v[j])
@@ -318,49 +339,44 @@
                     snd[n, both(p)] = part
                     partial_copy(p, n).start()
                 else:
-                    x_at = jnp.concatenate([x_v[pl.ds(lo, size), y_col(n - nh)],
-                                            x_v[pl.ds(nseq + lo, size), y_col(n - nh)]], 0)
+                    x_at = jnp.concatenate([x_v[seqs(p), y_col(n - nh)],
+                                            x_v[at_rows(nseq + p * SUB, SUB, SUB), y_col(n - nh)]], 0)
                     own[n - nh, both(p)] = part + x_at.astype(F32)
 
     def forward(h):
         to_far[h].wait_recv()
         pass_on[h].start()
 
-    def need(h):
-        if h == 0:
-            to_near.wait_recv()
-            for i in range(2):
-                kv_new_copy(i).wait_recv()
-        if h == 2:
-            forward(kvh - 1)
-        pass_on[h].wait_recv()
-
-    npass = len(PASSES)
-    for p in range(npass):
-        d0, d1 = starts[p] // per, (starts[p] + PASSES[p]) // per
-        if p == 0:
-            forward(0)
-            for d in range(d0, d1):
-                attend(d, 0)
+    for d in range(SUB // per):
+        forward(d)
+        attend(d, 0)
+        refill(d)
+        for j in range(nh * d, nh * (d + 1)):
+            wo_copy(j).start()
+    forward(2)
+    to_near.wait_recv()
+    for i in range(2):
+        kv_new_copy(i).wait_recv()
+    merge(0, (0, 1, 2), lambda h: pass_on[h].wait_recv())
+    forward(3)
+    pass_on[3].wait_recv()
+    merge(0, (3,))
+    project(0, True)
+
+    def one_pass(p, carry):
+        def step(d, cc):
+            attend(d, p * SUB)
+
+            @pl.when(2 * d + RING < ngrp)
+            def _():
                 refill(d)
-                if d < 2:
-                    for j in range(nh * d, nh * (d + 1)):
-                        wo_copy(j).start()
-                    forward(1 + d)
-            merge(p, need)
-        else:
-            def step(d, carry):
-                attend(d, starts[p])
-
-                @pl.when(2 * d + RING < ngrp)
-                def _():
-                    refill(d)
-                return carry
-            lax.fori_loop(d0, d1, step, 0)
-            merge(p, lambda h: None)
-        project(p)
-        if p > 0:
-            finish(p - 1)
+            return cc
+        lax.fori_loop(p * (SUB // per), (p + 1) * (SUB // per), step, 0)
+        merge(p, tuple(range(kvh)))
+        finish(p - 1)
+        project(p, False)
+        return carry
+    lax.fori_loop(1, npass, one_pass, 0)
     finish(npass - 1)
 
     for p in range(npass):
@@ -390,7 +406,7 @@
         slots = k_suffix.shape[1]
         heads = w_q.shape[1] // hd
         rows = slots * kvh
-        npass, nh = len(PASSES), model // 4 // CB
+        npass, nh = nseq // SUB, model // 4 // CB
         nw = heads * hd // 2 // CB + 2
         hpb = CB // hd
         dims = (nseq, model, heads, kvh, hd, slots)
@@ -414,13 +430,11 @@
                 pltpu.VMEM((2, hpb, nseq, hd), BF16),
                 pltpu.VMEM((4, kvh, 2, npos, hd), BF16),
                 pltpu.VMEM((PAD, rows), jnp.int32),
-                pltpu.VMEM((max(PASSES) * PAD, hd), F32),
-                pltpu.VMEM((max(PASSES) * PAD, hd), F32),
-                pltpu.VMEM((heads, 2 * nseq, hd), BF16),
+                pltpu.VMEM((SUB * PAD, hd), F32),
+                pltpu.VMEM((SUB * PAD, hd), F32),
                 pltpu.VMEM((nh, 2 * nseq, CB), F32),
                 pltpu.VMEM((nh, 2 * nseq, CB), F32),
                 pltpu.VMEM((nh, 2 * nseq, CB), F32),
-                pltpu.VMEM((nh, 2 * nseq, CB), BF16),
                 dma((3,)), dma((2,)), dma((2,)), dma((nw,)), dma((2 * nh,)), dma((RING, 2)),
                 dma((2, kvh)), dma((2, kvh)), dma((nw,)), dma((nw,)), dma((npass, kvh)), dma((npass, kvh)),
                 dma((npass, nh)), dma((npass, nh)), dma((3, npass, nh)), dma((3, npass, nh)),

time: 84.7 us -> 76.3 us (0.901)
  Pallas kernels: 82.1 us -> 73.7 us
    pallas_call x1, Pallas kernels: 82.1 us -> 73.7 us  [device_step(): pl.pallas_call(functools.partial(body, dims), out_shape=jax.ShapeDtypeStr...]
where the time goes in v5:
time: 76.3 us; the launch traced here: 76.1 us
  Pallas kernels  73.7 us (97%)
  local copies, waits for them, and re-layouts  2.46 us (3%)
    pallas_call x1, Pallas kernels, device_step(): pl.pallas_call(functools.partial(body, dims), out_shape=jax.ShapeDtypeStr...  73.7 us
    unnamed x1, local copies, waits for them, and re-layouts  2.46 us

profile of v5, /device:TPU:0, one launch (start us, length us, event | category | flops | bytes accessed | tf_op | source)
XLA Modules:
  0.0 76.1 jit_solution(14325229158612625450)
XLA Ops:
  0.0 73.7 %shard_map.100 = bf16[128,5120]{1,0:T(8,128)(2,1)} custom-call(bf16[128,5120]{1,0:T(8,128)(2,1)} %hid.1, bf16[5120,2560]{1,0:T(8,128)(2,1)} %wq.1, bf16[5120,512]{1,0:T(8,128)(2,1)} %wk.1, bf16[5120,512]{1,0:T(8,128)(2,1)} %wv.1, bf16[2560,5120]{1,0:T(8,128)(2,1)} %wo.1, bf16[1024,128]{1,0:T(8,128)(2,1)} %bitcast.6, bf16[1024,128]{1,0:T(8,128)(2,1)} %bitcast.7, ...), custom_call_target="tpu_custom_call" | custom-call | tf_op jit(solution)/shard_map/pallas_call | solution.py:415
  73.7 2.5 %copy.12 = bf16[128,5120]{1,0:T(8,128)(2,1)} copy(bf16[128,5120]{1,0:T(8,128)(2,1)} %shard_map.100) | data formatting | bytes 2621440

commit v6 on v5

--- a/solution.py
+++ b/solution.py
@@ -18,6 +18,7 @@
 GRP = 8
 RING = 4
 AHEAD = 3
+EARLY = ((0,), (1, 2), (3, 4))
 PAD = 24
 
 
@@ -313,8 +314,8 @@
                 remote(other, there, y_snd.at[1, p, j], y_rcv.at[1, p, j], diag),
                 remote(other, there, y_snd.at[2, p, j], y_rcv.at[2, p, j], near)]
 
-    def finish(p):
-        for j in range(nh):
+    def finish(p, blocks):
+        for j in blocks:
             partial_copy(p, j).wait_recv()
             y = (own[j, both(p)] + rcv[j, both(p)]).astype(BF16)
             ybuf[y_rows(p, j, 0, 2)] = y
@@ -363,6 +364,8 @@
     merge(0, (3,))
     project(0, True)
 
+    dgs = SUB // per
+
     def one_pass(p, carry):
         def step(d, cc):
             attend(d, p * SUB)
@@ -370,14 +373,22 @@
             @pl.when(2 * d + RING < ngrp)
             def _():
                 refill(d)
+
+            @pl.when(d == p * dgs)
+            def _():
+                finish(p - 1, EARLY[0])
+
+            @pl.when(d == p * dgs + 1)
+            def _():
+                finish(p - 1, EARLY[1])
             return cc
-        lax.fori_loop(p * (SUB // per), (p + 1) * (SUB // per), step, 0)
+        lax.fori_loop(p * dgs, (p + 1) * dgs, step, 0)
         merge(p, tuple(range(kvh)))
-        finish(p - 1)
+        finish(p - 1, EARLY[2])
         project(p, False)
         return carry
     lax.fori_loop(1, npass, one_pass, 0)
-    finish(npass - 1)
+    finish(npass - 1, range(nh))
 
     for p in range(npass):
         for j in range(nh):

time: 76.3 us -> 74 us (0.970)
  Pallas kernels: 73.7 us -> 71.4 us
    pallas_call x1, Pallas kernels: 73.7 us -> 71.4 us  [device_step(): pl.pallas_call(functools.partial(body, dims), out_shape=jax.ShapeDtypeStr...]
where the time goes in v6:
time: 74 us; the launch traced here: 73.9 us
  Pallas kernels  71.4 us (96%)
  local copies, waits for them, and re-layouts  2.46 us (3%)
    pallas_call x1, Pallas kernels, device_step(): pl.pallas_call(functools.partial(body, dims), out_shape=jax.ShapeDtypeStr...  71.4 us
    unnamed x1, local copies, waits for them, and re-layouts  2.46 us

profile of v6, /device:TPU:0, one launch (start us, length us, event | category | flops | bytes accessed | tf_op | source)
XLA Modules:
  0.0 73.9 jit_solution(1460059940050688320)
XLA Ops:
  0.0 71.4 %shard_map.100 = bf16[128,5120]{1,0:T(8,128)(2,1)} custom-call(bf16[128,5120]{1,0:T(8,128)(2,1)} %hid.1, bf16[5120,2560]{1,0:T(8,128)(2,1)} %wq.1, bf16[5120,512]{1,0:T(8,128)(2,1)} %wk.1, bf16[5120,512]{1,0:T(8,128)(2,1)} %wv.1, bf16[2560,5120]{1,0:T(8,128)(2,1)} %wo.1, bf16[1024,128]{1,0:T(8,128)(2,1)} %bitcast.6, bf16[1024,128]{1,0:T(8,128)(2,1)} %bitcast.7, ...), custom_call_target="tpu_custom_call" | custom-call | tf_op jit(solution)/shard_map/pallas_call | solution.py:426
  71.4 2.5 %copy.12 = bf16[128,5120]{1,0:T(8,128)(2,1)} copy(bf16[128,5120]{1,0:T(8,128)(2,1)} %shard_map.100) | data formatting | bytes 2621440

commit v7 on v6

--- a/solution.py
+++ b/solution.py
@@ -32,7 +32,7 @@
 
 def body(dims, hid, wq, wk, wv, wo, kp, vp, ks, vs, lens, out,
          x_v, w_v, wo_v, k_ring, v_ring, q2, qg, qs, kvn, kvs, kvp, key,
-         o2, m2, snd, rcv, own,
+         o2, m2, snd, rcv, own, out_v, out_sem,
          x_sem, p_sem, n_sem, w_sem, wo_sem, kv_sem, g_snd, g_rcv, q_snd, q_rcv, a_snd, a_rcv,
          f_snd, f_rcv, y_snd, y_rcv):
     nseq, model, heads, kvh, hd, slots = dims
@@ -154,7 +154,8 @@
         else:
             kv_new_copy(n - nq).start()
 
-    todo = [(0, n) for n in range(nw)] + [(nseq, n) for n in range(nw)]
+    order = [(0, range(nq)), (nseq, range(nq)), (0, range(nq, nw)), (nseq, range(nq, nw))]
+    todo = [(lo, n) for lo, part in order for n in part]
     for i in range(0, len(todo), 2):
         pair = todo[i:i + 2]
         for lo, n in pair:
@@ -308,7 +309,7 @@
         return pl.ds(pl.multiple_of(t * half + core * quart + j * CB, CB), CB)
 
     def y_copies(p, j):
-        there = out.at[seqs(p), y_col(j)]
+        there = out_v.at[seqs(p), y_col(j)]
         one, other = [ybuf.at[y_rows(p, j, side, 1)] for side in range(2)]
         return [remote(one, there, y_snd.at[0, p, j], y_rcv.at[0, p, j], mate),
                 remote(other, there, y_snd.at[1, p, j], y_rcv.at[1, p, j], diag),
@@ -321,7 +322,7 @@
             ybuf[y_rows(p, j, 0, 2)] = y
             for cp in y_copies(p, j):
                 cp.start()
-            out[seqs(p), y_col(j)] = y[:SUB]
+            out_v[seqs(p), y_col(j)] = y[:SUB]
 
     def project(p, first):
         for h in range(kvh):
@@ -390,13 +391,17 @@
     lax.fori_loop(1, npass, one_pass, 0)
     finish(npass - 1, range(nh))
 
+    out_copies = [pltpu.make_async_copy(out_v.at[seqs(p)], out.at[seqs(p)], out_sem.at[p]) for p in range(npass)]
     for p in range(npass):
         for j in range(nh):
             partial_copy(p, j).wait_send()
             for cp in y_copies(p, j):
                 cp.wait()
+        out_copies[p].start()
         for h in range(kvh):
             att_copy(p, h).wait_send()
+    for cp in out_copies:
+        cp.wait()
     for n in range(nq):
         q_copy(n).wait_send()
     for i in range(2):
@@ -427,7 +432,7 @@
             functools.partial(body, dims),
             out_shape=jax.ShapeDtypeStruct((nseq, model), BF16),
             in_specs=[hbm] * 9 + [pl.BlockSpec(memory_space=pltpu.SMEM)],
-            out_specs=pl.BlockSpec(memory_space=pltpu.VMEM),
+            out_specs=hbm,
             scratch_shapes=[
                 pltpu.VMEM((2 * nseq, model), BF16),
                 pltpu.VMEM((nw, model, CB), BF16),
@@ -446,6 +451,7 @@
                 pltpu.VMEM((nh, 2 * nseq, CB), F32),
                 pltpu.VMEM((nh, 2 * nseq, CB), F32),
                 pltpu.VMEM((nh, 2 * nseq, CB), F32),
+                pltpu.VMEM((nseq, model), BF16), dma((npass,)),
                 dma((3,)), dma((2,)), dma((2,)), dma((nw,)), dma((2 * nh,)), dma((RING, 2)),
                 dma((2, kvh)), dma((2, kvh)), dma((nw,)), dma((nw,)), dma((npass, kvh)), dma((npass, kvh)),
                 dma((npass, nh)), dma((npass, nh)), dma((3, npass, nh)), dma((3, npass, nh)),

time: 74 us -> 73.7 us (level)
  no operation moved by 1% of the time
where the time goes in v7:
time: 73.7 us; the launch traced here: 73.6 us
  Pallas kernels  71.1 us (96%)
  local copies, waits for them, and re-layouts  2.46 us (3%)
    pallas_call x1, Pallas kernels, device_step(): pl.pallas_call(functools.partial(body, dims), out_shape=jax.ShapeDtypeStr...  71.1 us
    unnamed x1, local copies, waits for them, and re-layouts  2.46 us

profile of v7, /device:TPU:0, one launch (start us, length us, event | category | flops | bytes accessed | tf_op | source)
XLA Modules:
  0.0 73.6 jit_solution(5721174014821889895)
XLA Ops:
  0.0 71.1 %shard_map.100 = bf16[128,5120]{1,0:T(8,128)(2,1)} custom-call(bf16[128,5120]{1,0:T(8,128)(2,1)} %hid.1, bf16[5120,2560]{1,0:T(8,128)(2,1)} %wq.1, bf16[5120,512]{1,0:T(8,128)(2,1)} %wk.1, bf16[5120,512]{1,0:T(8,128)(2,1)} %wv.1, bf16[2560,5120]{1,0:T(8,128)(2,1)} %wo.1, bf16[1024,128]{1,0:T(8,128)(2,1)} %bitcast.6, bf16[1024,128]{1,0:T(8,128)(2,1)} %bitcast.7, ...), custom_call_target="tpu_custom_call" | custom-call | tf_op jit(solution)/shard_map/pallas_call | solution.py:431
  71.1 2.5 %copy.12 = bf16[128,5120]{1,0:T(8,128)(2,1)} copy(bf16[128,5120]{1,0:T(8,128)(2,1)} %shard_map.100) | data formatting | bytes 2621440
